TPU v7x, 128 devices: a whole 4x4x4 slice. The times are simulated.
128 devices in a mesh: section: 8 (over y, core), sim: 16 (over z, x).
Axes of the slice: x: 4, y: 4, z: 4, core: 2. Of those that a mesh axis runs over, the one named last changes fastest.
Arguments:
- state: float32 [256, 64, 16384], P('section', None, 'sim'), may hold values from -60 to 60
- owner: int32 [256, 1], P('section'), may hold values from 0 to 15; in each aligned block of 32 rows (0 to 31, 32 to 63, ...) at most 4 rows name the same one
- counts: int32 [256], P('section'), may hold values from 4096 to 16384
Outputs:
- slab_mean: float32 [256, 64], P('section')
- slab_cov: float32 [256, 4096], P('section', 'sim')
- group_cov: float32 [128, 4096], P(('section', 'sim'))
- global_mean: float32 [64], replicated
- global_cov: float32 [64, 64], replicated
Inputs may be any that keep to these rules, and one draw needn't show every extreme that they name: Among the 32 slabs of one group, no owner is named by more than 4 slabs, and one owner is named by exactly 4 slabs in some or all groups.
All inputs are finite; a program needn't handle non-finite values.
Results may differ from a plain program's by a relative error of at most 0.0003.
Values sent between devices are 32-bit elements; how exact they have to be, the bound alone decides.
A program may use at most 64 MiB of HBM per device.

v0:
```python
import jax
import jax.numpy as jnp
from jax import lax
from jax.sharding import Mesh
from jax.sharding import PartitionSpec as P

SIM = ("sim_0", "sim_1")
SECTION_SIM = ("section_0", "section_1", "sim_0", "sim_1")
SECTION = ("section_0", "section_1")


def sent_to_all(value, axis):
    count = lax.axis_size(axis)
    return lax.all_to_all(
        jnp.broadcast_to(value[None], (count, *value.shape)), axis, 0, 0, tiled=True
    )


def taken_together(value, axis):
    return sent_to_all(value, axis).sum(axis=0)


def split_up(value, dim, count):
    before, after = (value.shape[:dim], value.shape[dim + 1 :])
    return jnp.moveaxis(value.reshape(*before, count, -1, *after), dim, 0)


def sum_at_owner(value, axis, dim):
    count = lax.axis_size(axis)
    pieces = lax.all_to_all(split_up(value, dim, count), axis, 0, 0, tiled=True)
    return jnp.sum(pieces, axis=0)


def by_axis(value, axes):
    far, near = axes
    return taken_together(taken_together(value, near), far)


def together(arrays, axis):
    ends = [0]
    for a in arrays:
        ends.append(ends[-1] + a.size)
    running = by_axis(jnp.concatenate([a.ravel() for a in arrays]), axis)
    return tuple((running[b:e].reshape(a.shape) for a, b, e in zip(arrays, ends, ends[1:])))


def local(state, owner, counts):
    high = lax.Precision.HIGHEST
    slab_here, width, cells_dev = state.shape
    n_sim = lax.axis_size(SIM)
    my_index = lax.axis_index(SIM)
    target = owner[:, 0]
    totals = counts.astype(jnp.float32)
    tile_start = my_index * cells_dev
    live = jnp.arange(cells_dev, dtype=jnp.int32)[None, :] + tile_start < counts[:, None]
    tile_sum = jnp.sum(jnp.where(live[:, None, :], state, 0.0), axis=2)
    slab_sum = taken_together(tile_sum, SIM)
    slab_mean = slab_sum / totals[:, None]
    centered = jnp.where(live[:, None, :], state - slab_mean[:, :, None], 0.0)
    tile_co = jnp.einsum("svc,swc->svw", centered, centered, precision=high).reshape(
        slab_here, width * width
    )
    slab_part = sum_at_owner(tile_co, SIM, 1)
    slab_cov = slab_part / (totals - 1.0)[:, None]
    member = (target[:, None] == jnp.arange(n_sim, dtype=jnp.int32)[None, :]).astype(jnp.float32)
    owner_terms = jnp.dot(member.T, tile_co, precision=high)
    own_terms = sum_at_owner(owner_terms, SIM, 0)[0]
    weight = jnp.where(target == my_index, totals, 0.0)
    group_count = jnp.sum(weight)
    group_mean = jnp.sum(weight[:, None] * slab_mean, axis=0) / jnp.maximum(group_count, 1.0)
    offset = slab_mean - group_mean[None, :]
    group_co = own_terms + jnp.einsum(
        "k,kv,kw->vw", weight, offset, offset, precision=high
    ).reshape(width * width)
    group_cov = (group_co / jnp.maximum(group_count - 1.0, 1.0))[None, :]
    total, weighted = together(
        (group_count, group_count * group_mean), ("section_0", ("section_1", "sim_0", "sim_1"))
    )
    global_mean = weighted / total
    gap = group_mean - global_mean
    spread = by_axis(
        group_co + group_count * jnp.outer(gap, gap).reshape(-1),
        (("section_0", "section_1"), ("sim_0", "sim_1")),
    )
    global_cov = (spread / (total - 1.0)).reshape(width, width)
    return (slab_mean, slab_cov, group_cov, global_mean, global_cov)


def solution(mesh):
    finer = Mesh(mesh.devices.reshape(4, 2, 4, 4), ("section_0", "section_1", "sim_0", "sim_1"))
    return jax.shard_map(
        local,
        mesh=finer,
        in_specs=(P(SECTION, None, SIM), P(SECTION, None), P(SECTION)),
        out_specs=(P(SECTION, None), P(SECTION, SIM), P(SECTION_SIM, None), P(), P()),
        check_vma=False,
    )
```

profile of v0, /device:TPU:1, one launch (start us, length us, event | category | flops | bytes accessed | tf_op | source)
XLA Modules:
  0.0 110.0 jit_solution(13462422381912311473)
XLA Ops:
  0.6 0.0 copy-start.1
  0.6 0.0 copy-start.2
  0.7 0.8 broadcast_compare_fusion
  1.5 4.1 %select_reduce_fusion = f32[32,64]{1,0:T(8,128)S(1)} fusion(f32[32,64,1024]{2,1,0:T(8,128)} %param.3, pred[32,1024]{1,0:T(8,128)(4,1)S(1)} %broadcast_compare_fusion), kind=kLoop, calls=%fused_computation.3 | loop fusion | flops 4192256 | bytes 8429568 | tf_op jit(solution)/shard_map/reduce_sum | solution.py:56
  5.6 0.8 reshape.152
  6.4 8.4 %all-to-all-start = ((f32[16,1,2048]{2,1,0:T(1,128)}), f32[16,1,2048]{2,1,0:T(1,128)S(1)}, u32[]{:S(2)}, u32[]{:S(2)}) async-start(f32[16,1,2048]{2,1,0:T(1,128)} %reshape.152), calls=%async_computation | async-start | bytes 262144 | tf_op jit(solution)/shard_map/all_to_all | solution.py:14
  14.8 0.0 copy-done.1
  14.9 0.0 copy-done.2
  14.9 0.6 fusion.14
  16.1 5.6 %all-to-all-done = f32[16,1,2048]{2,1,0:T(1,128)S(1)} async-done(((f32[16,1,2048]{2,1,0:T(1,128)}), f32[16,1,2048]{2,1,0:T(1,128)S(1)}, u32[]{:S(2)}, u32[]{:S(2)}) %all-to-all-start) | async-done | bytes 131104 | tf_op jit(solution)/shard_map/all_to_all | solution.py:14
  21.7 0.5 broadcast.79
  22.2 0.9 reduce.5
  23.2 0.1 reshape.153
  23.3 0.1 multiply_reduce_fusion
  23.4 0.0 copy-start
  23.4 0.7 broadcast_multiply_fusion
  24.1 0.7 pad_maximum_fusion
  24.8 0.6 broadcast_in_dim.34
  25.4 5.7 %all-to-all-start.3 = ((f32[32,1,65]{2,1,0:T(1,128)}), f32[32,1,65]{2,1,0:T(1,128)S(1)}, u32[]{:S(2)}, u32[]{:S(2)}) async-start(f32[32,1,65]{2,1,0:T(1,128)} %broadcast_in_dim.34), calls=%async_computation.3 | async-start | bytes 32768 | tf_op jit(solution)/shard_map/all_to_all | solution.py:14
  31.1 14.9 %fusion = f32[32,64,64]{2,1,0:T(8,128)S(1)} fusion(f32[32,64,1024]{2,1,0:T(8,128)} %param.3, f32[32,64]{1,0:T(8,128)S(1)} %get-tuple-element.12, pred[32,1024]{1,0:T(8,128)(4,1)S(1)} %broadcast_compare_fusion), kind=kOutput, calls=%fused_computation | convolution fusion | flops 1614807040 | bytes 8953856 | tf_op jit(solution)/shard_map/svc,swc->svw/dot_general | solution.py:60
  46.0 0.3 fusion.6
  46.4 0.4 reshape.146
  46.7 0.0 all-to-all-done.3
  46.7 0.6 broadcast_in_dim.35
  47.3 4.2 %all-to-all-start.4 = ((f32[4,1,65]{2,1,0:T(1,128)}), f32[4,1,65]{2,1,0:T(1,128)S(1)}, u32[]{:S(2)}, u32[]{:S(2)}) async-start(f32[4,1,65]{2,1,0:T(1,128)} %broadcast_in_dim.35), calls=%async_computation.4 | async-start | bytes 4096 | tf_op jit(solution)/shard_map/all_to_all | solution.py:14
  51.5 0.4 convolution_bitcast_fusion
  51.9 0.1 reshape.151
  52.0 1.0 copy.13
  52.9 2.6 %all-to-all-done.4 = f32[4,1,65]{2,1,0:T(1,128)S(1)} async-done(((f32[4,1,65]{2,1,0:T(1,128)}), f32[4,1,65]{2,1,0:T(1,128)S(1)}, u32[]{:S(2)}, u32[]{:S(2)}) %all-to-all-start.4) | async-done | bytes 1072 | tf_op jit(solution)/shard_map/all_to_all | solution.py:14
  55.6 6.7 %all-to-all-start.2 = ((f32[16,1,4096]{2,1,0:T(1,128)}), f32[16,1,4096]{2,1,0:T(1,128)S(1)}, u32[]{:S(2)}, u32[]{:S(2)}) async-start(f32[16,1,4096]{2,1,0:T(1,128)} %copy.13), calls=%async_computation.2 | async-start | bytes 524288 | tf_op jit(solution)/shard_map/all_to_all | solution.py:30
  62.3 0.6 fusion.13
  62.9 0.7 multiply_multiply_fusion
  63.6 0.1 mul.60
  63.7 6.1 %all-to-all-done.2 = f32[16,1,4096]{2,1,0:T(1,128)S(1)} async-done(((f32[16,1,4096]{2,1,0:T(1,128)}), f32[16,1,4096]{2,1,0:T(1,128)S(1)}, u32[]{:S(2)}, u32[]{:S(2)}) %all-to-all-start.2) | async-done | bytes 262176 | tf_op jit(solution)/shard_map/all_to_all | solution.py:30
  69.8 0.2 reduce_sum.95
  70.0 0.9 broadcast_in_dim.36
  70.9 3.5 %all-to-all-start.5 = ((f32[16,1,4096]{2,1,0:T(1,128)}), f32[16,1,4096]{2,1,0:T(1,128)S(1)}, u32[]{:S(2)}, u32[]{:S(2)}) async-start(f32[16,1,4096]{2,1,0:T(1,128)} %broadcast_in_dim.36), calls=%async_computation.5 | async-start | bytes 524288 | tf_op jit(solution)/shard_map/all_to_all | solution.py:14
  75.1 0.1 reshape.148
  75.2 0.3 reshape_reshape.3
  75.5 1.1 copy.21
  76.6 0.0 copy-done
  76.6 5.4 %all-to-all-done.5 = f32[16,1,4096]{2,1,0:T(1,128)S(1)} async-done(((f32[16,1,4096]{2,1,0:T(1,128)}), f32[16,1,4096]{2,1,0:T(1,128)S(1)}, u32[]{:S(2)}, u32[]{:S(2)}) %all-to-all-start.5) | async-done | bytes 262176 | tf_op jit(solution)/shard_map/all_to_all | solution.py:14
  82.1 3.6 %all-to-all-start.1 = ((f32[16,32,256]{2,1,0:T(8,128)}), f32[16,32,256]{2,1,0:T(8,128)S(1)}, u32[]{:S(2)}, u32[]{:S(2)}) async-start(f32[16,32,256]{2,1,0:T(8,128)} %bitcast.13), calls=%async_computation.1 | async-start | bytes 1048576 | tf_op jit(solution)/shard_map/all_to_all | solution.py:30
  85.7 0.6 add_divide_fusion
  86.3 0.2 reduce_sum.101
  86.5 8.2 %all-to-all-done.1 = f32[16,32,256]{2,1,0:T(8,128)S(1)} async-done(((f32[16,32,256]{2,1,0:T(8,128)}), f32[16,32,256]{2,1,0:T(8,128)S(1)}, u32[]{:S(2)}, u32[]{:S(2)}) %all-to-all-start.1) | async-done | bytes 524320 | tf_op jit(solution)/shard_map/all_to_all | solution.py:30
  94.7 0.7 broadcast_in_dim.37
  95.4 8.5 %all-to-all-start.6 = ((f32[8,1,4096]{2,1,0:T(1,128)}), f32[8,1,4096]{2,1,0:T(1,128)S(1)}, u32[]{:S(2)}, u32[]{:S(2)}) async-start(f32[8,1,4096]{2,1,0:T(1,128)} %broadcast_in_dim.37), calls=%async_computation.6 | async-start | bytes 262144 | tf_op jit(solution)/shard_map/all_to_all | solution.py:14
  104.0 0.7 broadcast_divide_fusion
  104.7 4.5 %all-to-all-done.6 = f32[8,1,4096]{2,1,0:T(1,128)S(1)} async-done(((f32[8,1,4096]{2,1,0:T(1,128)}), f32[8,1,4096]{2,1,0:T(1,128)S(1)}, u32[]{:S(2)}, u32[]{:S(2)}) %all-to-all-start.6) | async-done | bytes 131104 | tf_op jit(solution)/shard_map/all_to_all | solution.py:14
  109.2 0.1 reduce_sum.102
  109.3 0.7 div.71
  (9 shorter events, 0.2 us)
Async XLA Ops:
  0.6 14.2 %copy-start.1 = (s32[32]{0:T(128)S(1)}, s32[32]{0:T(128)}, u32[]{:S(2)}) copy-start(s32[32]{0:T(128)} %param.5) | copy-start | bytes 388
  0.6 14.2 %copy-start.2 = (s32[32,1]{0,1:T(1,128)S(1)}, s32[32,1]{0,1:T(1,128)}, u32[]{:S(2)}) copy-start(s32[32,1]{0,1:T(1,128)} %param.4) | copy-start | bytes 388
  6.4 15.3 %all-to-all-start = ((f32[16,1,2048]{2,1,0:T(1,128)}), f32[16,1,2048]{2,1,0:T(1,128)S(1)}, u32[]{:S(2)}, u32[]{:S(2)}) async-start(f32[16,1,2048]{2,1,0:T(1,128)} %reshape.152), calls=%async_computation | async-start | bytes 262144 | tf_op jit(solution)/shard_map/all_to_all | solution.py:14
  23.4 53.2 %copy-start = (f32[32,64]{1,0:T(8,128)}, f32[32,64]{1,0:T(8,128)S(1)}, u32[]{:S(2)}) copy-start(f32[32,64]{1,0:T(8,128)S(1)} %get-tuple-element.12) | copy-start | bytes 24580
  25.4 21.3 %all-to-all-start.3 = ((f32[32,1,65]{2,1,0:T(1,128)}), f32[32,1,65]{2,1,0:T(1,128)S(1)}, u32[]{:S(2)}, u32[]{:S(2)}) async-start(f32[32,1,65]{2,1,0:T(1,128)} %broadcast_in_dim.34), calls=%async_computation.3 | async-start | bytes 32768 | tf_op jit(solution)/shard_map/all_to_all | solution.py:14
  47.3 8.2 %all-to-all-start.4 = ((f32[4,1,65]{2,1,0:T(1,128)}), f32[4,1,65]{2,1,0:T(1,128)S(1)}, u32[]{:S(2)}, u32[]{:S(2)}) async-start(f32[4,1,65]{2,1,0:T(1,128)} %broadcast_in_dim.35), calls=%async_computation.4 | async-start | bytes 4096 | tf_op jit(solution)/shard_map/all_to_all | solution.py:14
  55.6 14.3 %all-to-all-start.2 = ((f32[16,1,4096]{2,1,0:T(1,128)}), f32[16,1,4096]{2,1,0:T(1,128)S(1)}, u32[]{:S(2)}, u32[]{:S(2)}) async-start(f32[16,1,4096]{2,1,0:T(1,128)} %copy.13), calls=%async_computation.2 | async-start | bytes 524288 | tf_op jit(solution)/shard_map/all_to_all | solution.py:30
  70.9 11.1 %all-to-all-start.5 = ((f32[16,1,4096]{2,1,0:T(1,128)}), f32[16,1,4096]{2,1,0:T(1,128)S(1)}, u32[]{:S(2)}, u32[]{:S(2)}) async-start(f32[16,1,4096]{2,1,0:T(1,128)} %broadcast_in_dim.36), calls=%async_computation.5 | async-start | bytes 524288 | tf_op jit(solution)/shard_map/all_to_all | solution.py:14
  82.1 12.6 %all-to-all-start.1 = ((f32[16,32,256]{2,1,0:T(8,128)}), f32[16,32,256]{2,1,0:T(8,128)S(1)}, u32[]{:S(2)}, u32[]{:S(2)}) async-start(f32[16,32,256]{2,1,0:T(8,128)} %bitcast.13), calls=%async_computation.1 | async-start | bytes 1048576 | tf_op jit(solution)/shard_map/all_to_all | solution.py:30
  95.4 13.8 %all-to-all-start.6 = ((f32[8,1,4096]{2,1,0:T(1,128)}), f32[8,1,4096]{2,1,0:T(1,128)S(1)}, u32[]{:S(2)}, u32[]{:S(2)}) async-start(f32[8,1,4096]{2,1,0:T(1,128)} %broadcast_in_dim.37), calls=%async_computation.6 | async-start | bytes 262144 | tf_op jit(solution)/shard_map/all_to_all | solution.py:14
where the time goes:
time: 111 us; the launch traced here: 110 us
  starting transfers between devices  40.6 us (37%)
  waiting for transfers between devices  32.5 us (29%)
  matrix products  15.6 us (14%)
  other arithmetic  11.2 us (10%)
  local copies, waits for them, and re-layouts  7.91 us (7%)
  between operations  2.18 us (2%)
    all_to_all x5, starting transfers between devices, sent_to_all(): lax.all_to_all(jnp.broadcast_to(value[None], (count, *value.shape)), axis...  30.3 us
    all_to_all x5, waiting for transfers between devices, sent_to_all(): lax.all_to_all(jnp.broadcast_to(value[None], (count, *value.shape)), axis...  18.2 us
    dot_general x1, matrix products, local(): jnp.einsum('svc,swc->svw', centered, centered, precision=high)  14.9 us
    all_to_all x2, waiting for transfers between devices, sum_at_owner(): pieces = lax.all_to_all(split_up(value, dim, count), axis, 0, 0, tiled=True)  14.3 us
    all_to_all x2, starting transfers between devices, sum_at_owner(): pieces = lax.all_to_all(split_up(value, dim, count), axis, 0, 0, tiled=True)  10.3 us
    reduce_sum x1, other arithmetic, local(): tile_sum = jnp.sum(jnp.where(live[:, None, :], state, 0.0), axis=2)  4.11 us
    broadcast_in_dim x5, local copies, waits for them, and re-layouts, sent_to_all(): jnp.broadcast_to(value[None], (count, *value.shape))  2.83 us
  transfers between devices with their start and end apart: 7, of which 6 were waited for; matrix products, arithmetic and copies ran while one was open for 20% of the time, Pallas kernels for 0%

commit v1 on v0

v1 whole, which is shorter than its diff:
```python
import functools

import jax
import jax.numpy as jnp
from jax import lax
from jax.experimental import pallas as pl
from jax.experimental.pallas import tpu as pltpu
from jax.sharding import PartitionSpec as P

MESH = pl.DeviceIdType.MESH
HIGH = lax.Precision.HIGHEST
F32 = jnp.float32
BF16 = jnp.bfloat16


def dot_rows(a, b):
    return lax.dot_general(a, b, (((1,), (1,)), ((), ())), preferred_element_type=F32)


def dot_high(a, b):
    return jnp.dot(a, b, precision=HIGH, preferred_element_type=F32)


def iota(shape, dim):
    return lax.broadcasted_iota(jnp.int32, shape, dim)


def kernel(
    n_sec, n_sim, width, chunks,
    state, counts, owner,
    mean_out, cov_out, grp_out, gmean_out, gcov_out,
    xv, meanb, cobuf, sums, sq, sendb, recvb, qbuf, qrecv, zrecv, frecv, gsend, grecv, grp, corrb, n64, own64, turn, turn2,
    load_sem, send_sem, sums_sem, piece_sem, q_sem, z_sem, f_sem, g_sem,
):
    pairs, _, cells = xv.shape
    half = pairs // 2
    sec = lax.axis_index("section")
    me = lax.axis_index("sim")
    z, x = me // 4, me % 4
    base = me * cells

    def sim_peer(k):
        return ((z + k // 4) % 4) * 4 + (x + k % 4) % 4

    def sec_peer(k):
        return (sec + k) % n_sec

    loads = [pltpu.make_async_copy(state.at[p], xv.at[p], load_sem.at[p]) for p in range(pairs)]
    for c in loads:
        c.start()

    barrier = pltpu.get_barrier_semaphore()
    for k in range(1, n_sim):
        pl.semaphore_signal(barrier, inc=1, device_id=(sec, sim_peer(k)), device_id_type=MESH)
    for k in range(1, n_sec):
        pl.semaphore_signal(barrier, inc=1, device_id=(sec_peer(k), me), device_id_type=MESH)

    lane8, sub8 = iota((8, 128), 1), iota((8, 128), 0)
    left8, first8 = lane8 < width, sub8 % 2 == 0
    for i in range(half):
        def spread(ref):
            return jnp.where(
                left8,
                jnp.where(first8, ref[4 * i], ref[4 * i + 2]),
                jnp.where(first8, ref[4 * i + 1], ref[4 * i + 3]),
            )
        n64[8 * i:8 * i + 8, :] = spread(counts).astype(F32)
        own64[8 * i:8 * i + 8, :] = spread(owner)
    lane16, sub16 = iota((pairs, 128), 1), iota((pairs, 128), 0)
    left16 = lane16 < width
    c_even = jnp.zeros((pairs, 128), jnp.int32)
    c_odd, o_even, o_odd = c_even, c_even, c_even
    for p in range(pairs):
        here = sub16 == p
        c_even = jnp.where(here, counts[2 * p], c_even)
        c_odd = jnp.where(here, counts[2 * p + 1], c_odd)
        o_even = jnp.where(here, owner[2 * p], o_even)
        o_odd = jnp.where(here, owner[2 * p + 1], o_odd)
    n_int = jnp.where(left16, c_even, c_odd)
    n_all = n_int.astype(F32)
    n_loc = jnp.clip(n_int - base, 0, cells).astype(F32)

    lane_c = iota((1, cells), 1)
    lane128 = iota((128, 128), 1)

    def first(p, cols):
        pltpu.make_async_copy(state.at[p], xv.at[p], load_sem.at[p]).wait()
        got = []
        for h in range(2):
            n = jnp.clip(counts[2 * p + h] - base, 0, cells)
            block = xv[p, h * width:(h + 1) * width, :]
            s = jnp.sum(jnp.where(lane_c < n, block, 0.0), axis=1, keepdims=True)
            s = jnp.broadcast_to(s, (width, 128))
            meanb[p, h * width:(h + 1) * width, :] = s / jnp.maximum(n, 1).astype(F32)
            got.append(s)
        return jnp.where(lane128 == p, jnp.concatenate(got, axis=0), cols)

    cols = lax.fori_loop(0, pairs, first, jnp.zeros((128, 128), F32))
    mine = cols.T[0:pairs, :]
    sums[me] = mine

    pl.semaphore_wait(barrier, n_sim - 1 + n_sec - 1)
    for k in range(1, n_sim):
        pltpu.make_async_remote_copy(
            sums.at[me], sums.at[me], send_sem.at[0], sums_sem,
            device_id=(sec, sim_peer(k)), device_id_type=MESH,
        ).start()

    left64 = iota((width, 128), 1) < width

    def second(p, carry):
        hi, lo = [], []
        for h in range(2):
            n = jnp.clip(counts[2 * p + h] - base, 0, cells)
            rows = pl.ds(h * width, width)
            m = meanb[p, rows, :]
            m = jnp.concatenate([m] * (cells // 128), axis=1)
            c = jnp.where(lane_c < n, xv[p, rows, :] - m, 0.0)
            top = c.astype(BF16)
            hi.append(top)
            lo.append((c - top.astype(F32)).astype(BF16))
        hi = jnp.concatenate(hi, axis=0)
        lo = jnp.concatenate(lo, axis=0)
        both = dot_rows(hi, jnp.concatenate([hi, lo], axis=0))
        cross = both[:, 128:256]
        full = both[:, 0:128] + cross + cross.T
        cobuf[p] = jnp.where(left64, full[0:width, :], full[width:, :])
        return carry

    lax.fori_loop(0, pairs, second, 0)

    pltpu.make_async_copy(sums.at[pl.ds(0, n_sim - 1)], sums.at[pl.ds(0, n_sim - 1)], sums_sem).wait()
    total = sums[0]
    for d in range(1, n_sim):
        total = total + sums[d]
    means = total / n_all
    shift = mine / jnp.maximum(n_loc, 1.0) - means
    sq[...] = jnp.zeros((128, 128), F32)
    sq[0:pairs, :] = shift
    col_shift = sq[...].T
    row_shift = shift * n_loc

    qsum = jnp.zeros((width, 128), F32)
    per = half // chunks
    for p in range(pairs):
        i, pp = p // 2, p % 2
        c = jnp.where(left64, col_shift[0:width, p:p + 1], col_shift[width:, p:p + 1])
        co = cobuf[p] + c * row_shift[p:p + 1, :]
        qsum = qsum + co
        sendb[i, pl.ds(pp, width, stride=2), :] = co
        if pp == 1 and (i + 1) % per == 0:
            t = i // per
            for k in range(1, n_sim):
                to = sim_peer(k)
                pltpu.make_async_remote_copy(
                    sendb.at[pl.ds(t * per, per), pl.ds(pl.multiple_of(8 * to, 8), 8), :],
                    recvb.at[me, pl.ds(t * per, per)],
                    send_sem.at[1], piece_sem.at[t],
                    device_id=(sec, to), device_id_type=MESH,
                ).start()
    recvb[me] = sendb[:, pl.ds(pl.multiple_of(8 * me, 8), 8), :]

    swapped = pltpu.roll(means, width, 1)
    m_even = jnp.where(left16, means, swapped)
    m_odd = jnp.where(left16, swapped, means)
    cf_even, cf_odd = c_even.astype(F32), c_odd.astype(F32)

    def about(w_even, w_odd, least):
        count = jnp.sum(w_even, axis=0, keepdims=True) + jnp.sum(w_odd, axis=0, keepdims=True)
        weighted = jnp.sum(w_even * m_even, axis=0, keepdims=True) + jnp.sum(w_odd * m_odd, axis=0, keepdims=True)
        mean = weighted / jnp.maximum(count, least)
        d_even, d_odd = m_even - mean, m_odd - mean
        off = jnp.concatenate([d_even, d_odd], axis=0)
        left = jnp.concatenate([w_even * d_even, w_odd * d_odd], axis=0)
        return count, weighted, dot_high(left.T, off)[0:width, :]

    sec_count, sec_sum, sec_co = about(cf_even, cf_odd, 1.0)
    q = qsum + pltpu.roll(qsum, width, 1) + sec_co * (1.0 / n_sim)
    rows8 = jnp.where(sub8 == 0, sec_sum, jnp.where(sub8 == 1, sec_count, 0.0))
    for s in range(n_sec):
        qbuf[s, 0:8, :] = q[8 * s:8 * s + 8, :]
        qbuf[s, 8:16, :] = rows8
    for k in range(1, n_sec):
        to = sec_peer(k)
        pltpu.make_async_remote_copy(
            qbuf.at[to], qrecv.at[sec], send_sem.at[2], q_sem,
            device_id=(to, me), device_id_type=MESH,
        ).start()
    qrecv[sec] = qbuf[sec]

    turn[pl.ds(0, pairs, stride=2), :] = means
    turn[pl.ds(1, pairs, stride=2), :] = swapped
    mean_out[...] = turn[:, 0:width]
    grp_count, _, grp_co = about(
        jnp.where(o_even == me, cf_even, 0.0), jnp.where(o_odd == me, cf_odd, 0.0), 1.0
    )
    corrb[...] = grp_co
    left32 = iota((width // 2, 128), 1) < width
    between = jnp.where(left32, corrb[pl.ds(0, width // 2, stride=2), :], corrb[pl.ds(1, width // 2, stride=2), :])
    lane64, sub64 = iota((width, 128), 1), iota((width, 128), 0)
    names = jnp.where(
        ((sub64 % 8) // 2 == (lane64 % width) // n_sim) & (own64[...] == lane64 % n_sim), 1.0, 0.0
    ).T
    gsend[...] = jnp.zeros((8 * n_sim, 128), F32)

    pltpu.make_async_copy(qrecv.at[pl.ds(0, n_sec - 1)], qrecv.at[pl.ds(0, n_sec - 1)], q_sem).wait()
    part = qrecv[0, 0:8, :]
    sec_sums, sec_counts = qrecv[0, 8:9, :], qrecv[0, 9:10, :]
    sums_l, counts_l = [sec_sums], [sec_counts]
    for s in range(1, n_sec):
        part = part + qrecv[s, 0:8, :]
        sums_l.append(qrecv[s, 8:9, :])
        counts_l.append(qrecv[s, 9:10, :])
    sec_sums, sec_counts = jnp.concatenate(sums_l, axis=0), jnp.concatenate(counts_l, axis=0)
    zrecv[me] = part
    for k in range(1, n_sim):
        pltpu.make_async_remote_copy(
            zrecv.at[me], zrecv.at[me], send_sem.at[3], z_sem,
            device_id=(sec, sim_peer(k)), device_id_type=MESH,
        ).start()
    all_count = jnp.sum(sec_counts, axis=0, keepdims=True)
    all_mean = jnp.sum(sec_sums, axis=0, keepdims=True) / all_count
    gap = sec_sums / sec_counts - all_mean
    spread_co = dot_high((sec_counts * gap).T, gap)[0:width, :]
    gmean_out[...] = all_mean

    for t in range(chunks):
        pltpu.make_async_copy(
            recvb.at[pl.ds(0, n_sim - 1), pl.ds(0, per)], recvb.at[pl.ds(0, n_sim - 1), pl.ds(0, per)],
            piece_sem.at[t],
        ).wait()
    co = recvb[0]
    for d in range(1, n_sim):
        co = co + recvb[d]
    co = co.reshape(width, 128)
    named = dot_high(names, co)
    g = jnp.where(left64, named[0:width, :], named[width:, :])
    g = g + pltpu.roll(g, width, 1)
    gsend[pl.ds(0, n_sim, stride=8), :] = jnp.where(left16, g[0:16, :], g[16:32, :])
    gsend[pl.ds(1, n_sim, stride=8), :] = jnp.where(left16, g[32:48, :], g[48:64, :])
    mine8 = pl.ds(pl.multiple_of(8 * me, 8), 8)
    for k in range(1, n_sim):
        to = sim_peer(k)
        pltpu.make_async_remote_copy(
            gsend.at[pl.ds(pl.multiple_of(8 * to, 8), 8), :], grecv.at[mine8, :], send_sem.at[4], g_sem,
            device_id=(sec, to), device_id_type=MESH,
        ).start()
    grecv[mine8, :] = gsend[mine8, :]

    corrb[...] = co / (n64[...] - 1.0)
    for pp in range(2):
        for rr in range(2):
            a = corrb[pl.ds(4 * rr + pp, 8, stride=8), :]
            b = corrb[pl.ds(4 * rr + 2 + pp, 8, stride=8), :]
            turned = turn if rr == 0 else turn2
            turned[pl.ds(2 * pp, 8, stride=4), :] = jnp.where(left8, a, pltpu.roll(b, width, 1))
            turned[pl.ds(2 * pp + 1, 8, stride=4), :] = jnp.where(left8, pltpu.roll(a, width, 1), b)
    cov_out[:, 0:128] = turn[...]
    cov_out[:, 128:256] = turn2[...]

    pltpu.make_async_copy(zrecv.at[pl.ds(0, n_sim - 1)], zrecv.at[pl.ds(0, n_sim - 1)], z_sem).wait()
    part = zrecv[0]
    for d in range(1, n_sim):
        part = part + zrecv[d]
    frecv[sec] = part
    for k in range(1, n_sec):
        pltpu.make_async_remote_copy(
            frecv.at[sec], frecv.at[sec], send_sem.at[5], f_sem,
            device_id=(sec_peer(k), me), device_id_type=MESH,
        ).start()

    pltpu.make_async_copy(
        grecv.at[pl.ds(0, 8 * (n_sim - 1)), :], grecv.at[pl.ds(0, 8 * (n_sim - 1)), :], g_sem
    ).wait()
    grp[pl.ds(0, n_sim, stride=2), :] = grecv[pl.ds(0, n_sim, stride=8), :]
    grp[pl.ds(1, n_sim, stride=2), :] = grecv[pl.ds(1, n_sim, stride=8), :]
    grp_out[...] = (grp[...] + between) / jnp.maximum(grp_count - 1.0, 1.0)

    pltpu.make_async_copy(frecv.at[pl.ds(0, n_sec - 1)], frecv.at[pl.ds(0, n_sec - 1)], f_sem).wait()
    whole = frecv[...].reshape(width, 128)
    gcov_out[...] = ((whole + spread_co) / (all_count - 1.0))[:, 0:width]

    def sent(ref, n, sem):
        pltpu.make_async_copy(ref.at[pl.ds(0, n)], ref.at[pl.ds(0, n)], sem).wait()

    sent(sums, n_sim - 1, send_sem.at[0])
    sent(recvb, n_sim - 1, send_sem.at[1])
    sent(qrecv, n_sec - 1, send_sem.at[2])
    sent(zrecv, n_sim - 1, send_sem.at[3])
    sent(grecv, 8 * (n_sim - 1), send_sem.at[4])
    sent(frecv, n_sec - 1, send_sem.at[5])


def solution(mesh):
    n_sec, n_sim = mesh.shape["section"], mesh.shape["sim"]
    chunks = 2

    def local(state, owner, counts):
        slabs, width, cells = state.shape
        pairs = slabs // 2
        half = pairs // 2
        vmem = pl.BlockSpec(memory_space=pltpu.VMEM)
        smem = pl.BlockSpec(memory_space=pltpu.SMEM)
        dma = pltpu.SemaphoreType.DMA
        mean, cov, grp, gmean, gcov = pl.pallas_call(
            functools.partial(kernel, n_sec, n_sim, width, chunks),
            out_shape=[
                jax.ShapeDtypeStruct((slabs, width), F32),
                jax.ShapeDtypeStruct((slabs, width * width // n_sim), F32),
                jax.ShapeDtypeStruct((width // 2, 2 * width), F32),
                jax.ShapeDtypeStruct((1, 2 * width), F32),
                jax.ShapeDtypeStruct((width, width), F32),
            ],
            in_specs=[pl.BlockSpec(memory_space=pl.ANY), smem, smem],
            out_specs=[vmem] * 5,
            scratch_shapes=[
                pltpu.VMEM((pairs, 2 * width, cells), F32),
                pltpu.VMEM((pairs, 2 * width, 128), F32),
                pltpu.VMEM((pairs, width, 128), F32),
                pltpu.VMEM((n_sim, pairs, 128), F32),
                pltpu.VMEM((128, 128), F32),
                pltpu.VMEM((half, 2 * width, 128), F32),
                pltpu.VMEM((n_sim, half, 8, 128), F32),
                pltpu.VMEM((n_sec, 16, 128), F32),
                pltpu.VMEM((n_sec, 16, 128), F32),
                pltpu.VMEM((n_sim, 8, 128), F32),
                pltpu.VMEM((n_sec, 8, 128), F32),
                pltpu.VMEM((8 * n_sim, 128), F32),
                pltpu.VMEM((8 * n_sim, 128), F32),
                pltpu.VMEM((width // 2, 128), F32),
                pltpu.VMEM((width, 128), F32),
                pltpu.VMEM((width, 128), F32),
                pltpu.VMEM((width, 128), jnp.int32),
                pltpu.VMEM((slabs, 128), F32),
                pltpu.VMEM((slabs, 128), F32),
                dma((pairs,)),
                dma((6,)),
                dma(()),
                dma((chunks,)),
                dma(()),
                dma(()),
                dma(()),
                dma(()),
            ],
            compiler_params=pltpu.CompilerParams(
                collective_id=0, has_side_effects=True, vmem_limit_bytes=32 * 1024 * 1024
            ),
            name="moments",
        )(state.reshape(pairs, 2 * width, cells), counts, owner.reshape(slabs))
        return mean, cov, grp.reshape(1, width * width), gmean[0, :width], gcov

    return jax.shard_map(
        local,
        mesh=mesh,
        in_specs=(P("section", None, "sim"), P("section", None), P("section")),
        out_specs=(P("section", None), P("section", "sim"), P(("section", "sim"), None), P(), P()),
        check_vma=False,
    )
```

time: 111 us -> 38.2 us (0.34)
  starting transfers between devices: 40.6 us -> 0 us
  waiting for transfers between devices: 32.5 us -> 0 us
  Pallas kernels: 0 us -> 29.8 us
  matrix products: 15.6 us -> 0 us
  other arithmetic: 11.2 us -> 0 us
  between operations: 2.18 us -> 0.65 us
    all_to_all x7 -> x0, starting transfers between devices: 40.6 us -> none  [the longest x5 30.3 us: sent_to_all(): lax.all_to_all(jnp.broadcast_to(value[None], (count, *value.shape)), axis...]
    all_to_all x7 -> x0, waiting for transfers between devices: 32.5 us -> none  [the longest x5 18.2 us: sent_to_all(): lax.all_to_all(jnp.broadcast_to(value[None], (count, *value.shape)), axis...]
    pallas_call x0 -> x1, Pallas kernels: none -> 29.8 us  [local(): pl.pallas_call(functools.partial(kernel, n_sec, n_sim, width, chunks), ou...]
    dot_general x3 -> x0, matrix products: 15.6 us -> none  [the longest x1 14.9 us: local(): jnp.einsum('svc,swc->svw', centered, centered, precision=high)]
    unnamed x8 -> x10, local copies, waits for them, and re-layouts: 0.94 us -> 7.12 us
    reduce_sum x10 -> x0, other arithmetic: 5.37 us -> none  [the longest x1 4.11 us: local(): tile_sum = jnp.sum(jnp.where(live[:, None, :], state, 0.0), axis=2)]
    broadcast_in_dim x5 -> x0, local copies, waits for them, and re-layouts: 2.83 us -> none  [sent_to_all(): jnp.broadcast_to(value[None], (count, *value.shape))]
    reshape x4 -> x0, local copies, waits for them, and re-layouts: 1.48 us -> none  [the longest x1 0.96 us: split_up(): return jnp.moveaxis(value.reshape(*before, count, -1, *after), dim, 0)]
  transfers between devices with their start and end apart: 7 -> 0, of which waited for: 6 -> 0; matrix products, arithmetic and copies ran while one was open for 20% -> 0% of each run, Pallas kernels for 0% -> 0%
where the time goes in v1:
time: 38.2 us; the launch traced here: 38.1 us
  Pallas kernels  29.8 us (78%)
  local copies, waits for them, and re-layouts  7.64 us (20%)
  between operations  0.65 us (2%)
    pallas_call x1, Pallas kernels, local(): pl.pallas_call(functools.partial(kernel, n_sec, n_sim, width, chunks), ou...  29.8 us
    unnamed x10, local copies, waits for them, and re-layouts  7.12 us

profile of v1, /device:TPU:1, one launch (start us, length us, event | category | flops | bytes accessed | tf_op | source)
XLA Modules:
  0.0 38.1 jit_solution(4099002989872531968)
XLA Ops:
  0.6 0.0 copy-start
  0.6 3.4 %copy-done = f32[32,64,1024]{2,1,0:T(8,128)S(1)} copy-done((f32[32,64,1024]{2,1,0:T(8,128)S(1)}, f32[32,64,1024]{2,1,0:T(8,128)}, u32[]{:S(2)}) %copy-start) | copy-done | bytes 8388632
  4.0 0.0 copy-start.1
  4.0 0.7 %copy-done.1 = s32[32]{0:T(128)S(1)} copy-done((s32[32]{0:T(128)S(1)}, s32[32]{0:T(128)}, u32[]{:S(2)}) %copy-start.1) | copy-done | bytes 152
  4.7 0.0 copy-start.2
  4.7 0.7 %copy-done.2 = s32[32,1]{0,1:T(1,128)S(1)} copy-done((s32[32,1]{0,1:T(1,128)S(1)}, s32[32,1]{0,1:T(1,128)}, u32[]{:S(2)}) %copy-start.2) | copy-done | bytes 152
  5.3 29.8 %moments.1 = (f32[32,64]{1,0:T(8,128)S(1)}, f32[32,256]{1,0:T(8,128)S(1)}, f32[32,128]{1,0:T(8,128)S(1)}, f32[1,128]{1,0:T(1,128)S(1)}, f32[64,64]{1,0:T(8,128)S(1)}) custom-call(f32[16,128,1024]{2,1,0:T(8,128)S(1)} %bitcast.5, s32[32]{0:T(128)S(1)} %copy-done.1, s32[32]{0:T(128)S(1)} %bitcast.7), custom_call_target="tpu_custom_call" | custom-call | tf_op jit(solution)/shard_map/moments/pallas_call | solution.py:305
  35.1 0.5 %slice_bitcast_fusion = f32[64]{0:T(128)} fusion(f32[1,128]{1,0:T(1,128)S(1)} %get-tuple-element.13), kind=kLoop, calls=%fused_computation | loop fusion | bytes 512 | tf_op jit(solution)/shard_map/squeeze | solution.py:350
  35.6 0.6 %copy.12 = f32[32,64]{1,0:T(8,128)} copy(f32[32,64]{1,0:T(8,128)S(1)} %get-tuple-element.20) | data formatting | bytes 16384
  36.2 0.6 %copy.13 = f32[32,256]{1,0:T(8,128)} copy(f32[32,256]{1,0:T(8,128)S(1)} %get-tuple-element.21) | data formatting | bytes 65536
  36.8 0.6 %copy.14 = f32[1,4096]{1,0:T(1,128)} copy(f32[1,4096]{1,0:T(1,128)S(1)} %bitcast.6) | data formatting | bytes 32768
  37.4 0.6 %copy.15 = f32[64,64]{1,0:T(8,128)} copy(f32[64,64]{1,0:T(8,128)S(1)} %get-tuple-element.24) | data formatting | bytes 32768
Async XLA Ops:
  0.6 3.4 %copy-start = (f32[32,64,1024]{2,1,0:T(8,128)S(1)}, f32[32,64,1024]{2,1,0:T(8,128)}, u32[]{:S(2)}) copy-start(f32[32,64,1024]{2,1,0:T(8,128)} %param.3) | copy-start | bytes 25165828
  4.0 0.7 %copy-start.1 = (s32[32]{0:T(128)S(1)}, s32[32]{0:T(128)}, u32[]{:S(2)}) copy-start(s32[32]{0:T(128)} %counts.1) | copy-start | bytes 388
  4.7 0.7 %copy-start.2 = (s32[32,1]{0,1:T(1,128)S(1)}, s32[32,1]{0,1:T(1,128)}, u32[]{:S(2)}) copy-start(s32[32,1]{0,1:T(1,128)} %param.4) | copy-start | bytes 388

commit v2 on v1

--- a/solution.py
+++ b/solution.py
@@ -27,10 +27,10 @@
 
 def kernel(
     n_sec, n_sim, width, chunks,
-    state, counts, owner,
+    state, counts_hbm, owner_hbm,
     mean_out, cov_out, grp_out, gmean_out, gcov_out,
     xv, meanb, cobuf, sums, sq, sendb, recvb, qbuf, qrecv, zrecv, frecv, gsend, grecv, grp, corrb, n64, own64, turn, turn2,
-    load_sem, send_sem, sums_sem, piece_sem, q_sem, z_sem, f_sem, g_sem,
+    counts, owner, load_sem, int_sem, send_sem, sums_sem, piece_sem, q_sem, z_sem, f_sem, g_sem,
 ):
     pairs, _, cells = xv.shape
     half = pairs // 2
@@ -46,7 +46,11 @@
         return (sec + k) % n_sec
 
     loads = [pltpu.make_async_copy(state.at[p], xv.at[p], load_sem.at[p]) for p in range(pairs)]
-    for c in loads:
+    small = [
+        pltpu.make_async_copy(counts_hbm, counts, int_sem.at[0]),
+        pltpu.make_async_copy(owner_hbm, owner, int_sem.at[1]),
+    ]
+    for c in small + loads:
         c.start()
 
     barrier = pltpu.get_barrier_semaphore()
@@ -54,6 +58,9 @@
         pl.semaphore_signal(barrier, inc=1, device_id=(sec, sim_peer(k)), device_id_type=MESH)
     for k in range(1, n_sec):
         pl.semaphore_signal(barrier, inc=1, device_id=(sec_peer(k), me), device_id_type=MESH)
+
+    for c in small:
+        c.wait()
 
     lane8, sub8 = iota((8, 128), 1), iota((8, 128), 0)
     left8, first8 = lane8 < width, sub8 % 2 == 0
@@ -222,7 +229,7 @@
     all_mean = jnp.sum(sec_sums, axis=0, keepdims=True) / all_count
     gap = sec_sums / sec_counts - all_mean
     spread_co = dot_high((sec_counts * gap).T, gap)[0:width, :]
-    gmean_out[...] = all_mean
+    gmean_out[...] = all_mean[:, 0:width]
 
     for t in range(chunks):
         pltpu.make_async_copy(
@@ -291,6 +298,15 @@
     sent(frecv, n_sec - 1, send_sem.at[5])
 
 
+def put(n, *refs):
+    ins, outs, sem = refs[:n], refs[n:2 * n], refs[2 * n]
+    copies = [pltpu.make_async_copy(a, b, sem.at[i]) for i, (a, b) in enumerate(zip(ins, outs))]
+    for c in copies:
+        c.start()
+    for c in copies:
+        c.wait()
+
+
 def solution(mesh):
     n_sec, n_sim = mesh.shape["section"], mesh.shape["sim"]
     chunks = 2
@@ -302,16 +318,18 @@
         vmem = pl.BlockSpec(memory_space=pltpu.VMEM)
         smem = pl.BlockSpec(memory_space=pltpu.SMEM)
         dma = pltpu.SemaphoreType.DMA
-        mean, cov, grp, gmean, gcov = pl.pallas_call(
+        hbm = pl.BlockSpec(memory_space=pltpu.HBM)
+        shapes = [
+            jax.ShapeDtypeStruct((slabs, width), F32),
+            jax.ShapeDtypeStruct((slabs, width * width // n_sim), F32),
+            jax.ShapeDtypeStruct((width // 2, 2 * width), F32),
+            jax.ShapeDtypeStruct((1, width), F32),
+            jax.ShapeDtypeStruct((width, width), F32),
+        ]
+        found = pl.pallas_call(
             functools.partial(kernel, n_sec, n_sim, width, chunks),
-            out_shape=[
-                jax.ShapeDtypeStruct((slabs, width), F32),
-                jax.ShapeDtypeStruct((slabs, width * width // n_sim), F32),
-                jax.ShapeDtypeStruct((width // 2, 2 * width), F32),
-                jax.ShapeDtypeStruct((1, 2 * width), F32),
-                jax.ShapeDtypeStruct((width, width), F32),
-            ],
-            in_specs=[pl.BlockSpec(memory_space=pl.ANY), smem, smem],
+            out_shape=shapes,
+            in_specs=[hbm] * 3,
             out_specs=[vmem] * 5,
             scratch_shapes=[
                 pltpu.VMEM((pairs, 2 * width, cells), F32),
@@ -333,7 +351,10 @@
                 pltpu.VMEM((width, 128), jnp.int32),
                 pltpu.VMEM((slabs, 128), F32),
                 pltpu.VMEM((slabs, 128), F32),
+                pltpu.SMEM((slabs,), jnp.int32),
+                pltpu.SMEM((slabs,), jnp.int32),
                 dma((pairs,)),
+                dma((2,)),
                 dma((6,)),
                 dma(()),
                 dma((chunks,)),
@@ -346,8 +367,20 @@
                 collective_id=0, has_side_effects=True, vmem_limit_bytes=32 * 1024 * 1024
             ),
             name="moments",
-        )(state.reshape(pairs, 2 * width, cells), counts, owner.reshape(slabs))
-        return mean, cov, grp.reshape(1, width * width), gmean[0, :width], gcov
+        )(*(
+            pltpu.with_memory_space_constraint(a, pltpu.HBM)
+            for a in (state.reshape(pairs, 2 * width, cells), counts, owner.reshape(slabs))
+        ))
+        mean, cov, grp, gmean, gcov = pl.pallas_call(
+            functools.partial(put, 5),
+            out_shape=shapes,
+            in_specs=[vmem] * 5,
+            out_specs=[hbm] * 5,
+            scratch_shapes=[dma((5,))],
+            compiler_params=pltpu.CompilerParams(vmem_limit_bytes=4 * 1024 * 1024),
+            name="put",
+        )(*found)
+        return mean, cov, grp.reshape(1, width * width), gmean.reshape(width), gcov
 
     return jax.shard_map(
         local,

time: 38.2 us -> 31.4 us (0.82)
  local copies, waits for them, and re-layouts: 7.64 us -> 0 us
  Pallas kernels: 29.8 us -> 30.7 us
    unnamed x10 -> x0, local copies, waits for them, and re-layouts: 7.12 us -> none
    pallas_call x0 -> x1, Pallas kernels: none -> 0.69 us  [local(): pl.pallas_call(functools.partial(put, 5), out_shape=shapes, in_specs=[vme...]
    squeeze x1 -> x0, local copies, waits for them, and re-layouts: 0.51 us -> none  [local(): return (mean, cov, grp.reshape(1, width * width), gmean[0, :width], gcov)]
where the time goes in v2:
time: 31.4 us; the launch traced here: 31.3 us
  Pallas kernels  30.7 us (98%)
  between operations  0.64 us (2%)
    pallas_call x1, Pallas kernels, local(): pl.pallas_call(functools.partial(kernel, n_sec, n_sim, width, chunks), ou...  30 us
    pallas_call x1, Pallas kernels, local(): pl.pallas_call(functools.partial(put, 5), out_shape=shapes, in_specs=[vme...  0.69 us

profile of v2, /device:TPU:1, one launch (start us, length us, event | category | flops | bytes accessed | tf_op | source)
XLA Modules:
  0.0 31.3 jit_solution(6455507056987202608)
XLA Ops:
  0.6 30.0 %moments.1 = (f32[32,64]{1,0:T(8,128)S(1)}, f32[32,256]{1,0:T(8,128)S(1)}, f32[32,128]{1,0:T(8,128)S(1)}, f32[1,64]{1,0:T(1,128)S(1)}, f32[64,64]{1,0:T(8,128)S(1)}) custom-call(f32[16,128,1024]{2,1,0:T(8,128)} %bitcast.4, s32[32]{0:T(128)} %counts_hbm.1, s32[32]{0:T(128)} %bitcast.5), custom_call_target="tpu_custom_call" | custom-call | tf_op jit(solution)/shard_map/moments/pallas_call | solution.py:329
  30.6 0.7 %put.1 = (f32[32,64]{1,0:T(8,128)}, f32[32,256]{1,0:T(8,128)}, f32[32,128]{1,0:T(8,128)}, f32[1,64]{1,0:T(1,128)}, f32[64,64]{1,0:T(8,128)}) custom-call(f32[32,64]{1,0:T(8,128)S(1)} %get-tuple-element.15.refs_0_, f32[32,256]{1,0:T(8,128)S(1)} %get-tuple-element.16.refs_1_, f32[32,128]{1,0:T(8,128)S(1)} %get-tuple-element.17.refs_2_, ...), custom_call_target="tpu_custom_call" | custom-call | tf_op jit(solution)/shard_map/put/pallas_call | solution.py:374

commit v3 on v2

v3 whole, which is shorter than its diff:
```python
import functools

import jax
import jax.numpy as jnp
from jax import lax
from jax.experimental import pallas as pl
from jax.experimental.pallas import tpu as pltpu
from jax.sharding import PartitionSpec as P

MESH = pl.DeviceIdType.MESH
HIGH = lax.Precision.HIGHEST
F32 = jnp.float32
BF16 = jnp.bfloat16


def dot_rows(a, b):
    return lax.dot_general(a, b, (((1,), (1,)), ((), ())), preferred_element_type=F32)


def dot_high(a, b):
    return jnp.dot(a, b, precision=HIGH, preferred_element_type=F32)


def iota(shape, dim):
    return lax.broadcasted_iota(jnp.int32, shape, dim)


def kernel(
    n_sec, n_sim, width, chunks,
    state, counts_hbm, owner_hbm,
    mean_out, cov_out, grp_out, gmean_out, gcov_out,
    xv, split, colsum, sums, sendb, recvb, qbuf, qrecv, zrecv, frecv, gsend, grecv, grp, corrb, n64, own64, turn, turn2,
    counts, owner, load_sem, int_sem, send_sem, sums_sem, piece_sem, q_sem, z_sem, f_sem, g_sem,
):
    pairs, _, cells = xv.shape
    half = pairs // 2
    sec = lax.axis_index("section")
    me = lax.axis_index("sim")
    z, x = me // 4, me % 4
    base = me * cells

    def sim_peer(k):
        return ((z + k // 4) % 4) * 4 + (x + k % 4) % 4

    def sec_peer(k):
        return (sec + k) % n_sec

    def block(i):
        return pl.ds(pl.multiple_of(8 * i, 8), 8)

    def double(i):
        return pl.ds(pl.multiple_of(16 * i, 16), 16)

    def arrived(ref, n, sem):
        pltpu.make_async_copy(ref.at[pl.ds(0, n)], ref.at[pl.ds(0, n)], sem).wait()

    small = [
        pltpu.make_async_copy(counts_hbm, counts, int_sem.at[0]),
        pltpu.make_async_copy(owner_hbm, owner, int_sem.at[1]),
    ]
    loads = {
        p: pltpu.make_async_copy(state.at[p], xv.at[p], load_sem.at[p])
        for i in range(half) for p in (i, i + half)
    }
    for c in small + list(loads.values()):
        c.start()

    barrier = pltpu.get_barrier_semaphore()
    for k in range(1, n_sim):
        pl.semaphore_signal(barrier, inc=1, device_id=(sec, sim_peer(k)), device_id_type=MESH)
    for k in range(1, n_sec):
        pl.semaphore_signal(barrier, inc=1, device_id=(sec_peer(k), me), device_id_type=MESH)

    for c in small:
        c.wait()

    lane8, sub8 = iota((8, 128), 1), iota((8, 128), 0)
    left8, first8 = lane8 < width, sub8 % 2 == 0
    for i in range(half):
        def spread(ref):
            return jnp.where(
                left8,
                jnp.where(first8, ref[2 * i], ref[2 * (i + half)]),
                jnp.where(first8, ref[2 * i + 1], ref[2 * (i + half) + 1]),
            )
        n64[8 * i:8 * i + 8, :] = spread(counts).astype(F32)
        own64[8 * i:8 * i + 8, :] = spread(owner)
    lane16, sub16 = iota((pairs, 128), 1), iota((pairs, 128), 0)
    left16 = lane16 < width
    c_even = jnp.zeros((pairs, 128), jnp.int32)
    c_odd, o_even, o_odd = c_even, c_even, c_even
    for p in range(pairs):
        here = sub16 == p
        c_even = jnp.where(here, counts[2 * p], c_even)
        c_odd = jnp.where(here, counts[2 * p + 1], c_odd)
        o_even = jnp.where(here, owner[2 * p], o_even)
        o_odd = jnp.where(here, owner[2 * p + 1], o_odd)
    n_int = jnp.where(left16, c_even, c_odd)
    colsum[...] = jnp.zeros((128, 128), F32)
    gsend[...] = jnp.zeros((8 * n_sim, 128), F32)

    lane_c = iota((1, cells), 1)
    left64 = iota((width, 128), 1) < width

    def centre(i):
        for pp in range(2):
            p = i + half * pp
            loads[p].wait()
        for pp in range(2):
            p = i + half * pp
            for h in range(2):
                n = jnp.clip(counts[2 * p + h] - base, 0, cells)
                live = lane_c < n
                cell = xv[p, h * width:(h + 1) * width, :]
                s = jnp.sum(jnp.where(live, cell, 0.0), axis=1, keepdims=True)
                colsum[h * width:(h + 1) * width, p:p + 1] = s
                m = s / jnp.maximum(n, 1).astype(F32)
                c = jnp.where(live, cell - m, 0.0)
                top = c.astype(BF16)
                split[i % 2, pp, h * width:(h + 1) * width, :] = top
                split[i % 2, pp, (2 + h) * width:(3 + h) * width, :] = (c - top.astype(F32)).astype(BF16)

    def multiply(i, qsum):
        for pp in range(2):
            both = dot_rows(split[i % 2, pp, 0:2 * width, :], split[i % 2, pp])
            cross = both[:, 128:256]
            full = both[:, 0:128] + cross + cross.T
            co = jnp.where(left64, full[0:width, :], full[width:, :])
            qsum = qsum + co
            sendb[i, pl.ds(pp, width, stride=2), :] = co
        return qsum

    per = half // chunks
    qsum = jnp.zeros((width, 128), F32)
    for i in range(half + 1):
        if i < half:
            centre(i)
        if i > 0:
            qsum = multiply(i - 1, qsum)
        if i > 0 and i % per == 0:
            t = i // per - 1
            if t == 0:
                pl.semaphore_wait(barrier, n_sim - 1 + n_sec - 1)
            for k in range(1, n_sim):
                to = sim_peer(k)
                pltpu.make_async_remote_copy(
                    sendb.at[pl.ds(t * per, per), block(to), :],
                    recvb.at[me, pl.ds(t * per, per)],
                    send_sem.at[1], piece_sem.at[t],
                    device_id=(sec, to), device_id_type=MESH,
                ).start()
    mine = colsum[...].T[0:pairs, :]
    sums[me] = mine
    for k in range(1, n_sim):
        pltpu.make_async_remote_copy(
            sums.at[me], sums.at[me], send_sem.at[0], sums_sem,
            device_id=(sec, sim_peer(k)), device_id_type=MESH,
        ).start()
    recvb[me] = sendb[:, block(me), :]

    def both_sides(value):
        turned = pltpu.roll(value, width, 1)
        return jnp.where(left16, value, turned), jnp.where(left16, turned, value)

    def about(m_even, m_odd, w_even, w_odd):
        count = jnp.sum(w_even + w_odd, axis=0, keepdims=True)
        mean = jnp.sum(w_even * m_even + w_odd * m_odd, axis=0, keepdims=True) / jnp.maximum(count, 1.0)
        d_even, d_odd = m_even - mean, m_odd - mean
        off = jnp.concatenate([d_even, d_odd], axis=0)
        left = jnp.concatenate([w_even * d_even, w_odd * d_odd], axis=0)
        return count, mean, dot_high(left.T, off)[0:width, :]

    def here(c, d):
        return jnp.clip(c - d * cells, 0, cells).astype(F32)

    n_mine = here(n_int, me)
    l_even, l_odd = both_sides(mine / jnp.maximum(n_mine, 1.0))
    dev_count, dev_mean, dev_co = about(l_even, l_odd, here(c_even, me), here(c_odd, me))
    q = qsum + pltpu.roll(qsum, width, 1) + dev_co
    rows8 = jnp.where(sub8 == 0, dev_mean, jnp.where(sub8 == 1, dev_count, 0.0))
    for s in range(n_sec):
        qbuf[16 * s:16 * s + 8, :] = q[8 * s:8 * s + 8, :]
        qbuf[16 * s + 8:16 * s + 16, :] = rows8
    for k in range(1, n_sec):
        to = sec_peer(k)
        pltpu.make_async_remote_copy(
            qbuf.at[double(to), :], qrecv.at[double(sec), :], send_sem.at[2], q_sem,
            device_id=(to, me), device_id_type=MESH,
        ).start()
    qrecv[double(sec), :] = qbuf[double(sec), :]

    lane64, sub64 = iota((width, 128), 1), iota((width, 128), 0)
    names = jnp.where(
        ((sub64 % 8) // 2 == (lane64 % width) // n_sim) & (own64[...] == lane64 % n_sim), 1.0, 0.0
    ).T

    def merged(ref, n):
        part = ref[0:8, :]
        for s in range(1, n):
            part = part + ref[16 * s:16 * s + 8, :]
        means = ref[pl.ds(8, n, stride=16), :]
        weights = ref[pl.ds(9, n, stride=16), :]
        count = jnp.sum(weights, axis=0, keepdims=True)
        mean = jnp.sum(weights * means, axis=0, keepdims=True) / jnp.maximum(count, 1.0)
        gap = means - mean
        corrb[...] = dot_high((weights * gap).T, gap)[0:width, :]
        return part + corrb[block(sec), :], mean, count

    arrived(qrecv, 16 * (n_sec - 1), q_sem)
    part, part_mean, part_count = merged(qrecv, n_sec)
    own_z = double(me)
    zrecv[own_z, :] = jnp.concatenate(
        [part, jnp.where(sub8 == 0, part_mean, jnp.where(sub8 == 1, part_count, 0.0))], axis=0
    )
    for k in range(1, n_sim):
        pltpu.make_async_remote_copy(
            zrecv.at[own_z, :], zrecv.at[own_z, :], send_sem.at[3], z_sem,
            device_id=(sec, sim_peer(k)), device_id_type=MESH,
        ).start()

    arrived(sums, n_sim - 1, sums_sem)
    total = sums[0]
    for d in range(1, n_sim):
        total = total + sums[d]
    means = total / n_int.astype(F32)
    turn[pl.ds(0, pairs, stride=2), :] = means
    turn[pl.ds(1, pairs, stride=2), :] = pltpu.roll(means, width, 1)
    mean_out[...] = turn[:, 0:width]

    rows = [jnp.zeros((pairs, 128), F32) for _ in range(4)]
    to_front = (128 - 4 * me) % 128
    for d in range(n_sim):
        n = here(n_int, d)
        gap = sums[d] / jnp.maximum(n, 1.0) - means
        front = pltpu.roll(gap, to_front, 1)
        gap_n = gap * n
        for r in range(4):
            rows[r] = rows[r] + jnp.where(left16, front[:, r:r + 1], front[:, width + r:width + r + 1]) * gap_n
    for r in range(4):
        for pp in range(2):
            corrb[pl.ds(2 * r + pp, half, stride=8), :] = rows[r][half * pp:half * (pp + 1), :]
    co = corrb[...]
    m_even, m_odd = both_sides(means)
    grp_count, _, grp_co = about(
        m_even, m_odd,
        jnp.where(o_even == me, c_even, 0).astype(F32), jnp.where(o_odd == me, c_odd, 0).astype(F32),
    )
    corrb[...] = grp_co
    left32 = iota((width // 2, 128), 1) < width
    between = jnp.where(left32, corrb[pl.ds(0, width // 2, stride=2), :], corrb[pl.ds(1, width // 2, stride=2), :])

    for t in range(chunks):
        few = recvb.at[pl.ds(0, n_sim - 1), pl.ds(0, per)]
        pltpu.make_async_copy(few, few, piece_sem.at[t]).wait()
    for d in range(n_sim):
        co = co + recvb[d].reshape(width, 128)
    named = dot_high(names, co)
    g = jnp.where(left64, named[0:width, :], named[width:, :])
    g = g + pltpu.roll(g, width, 1)
    gsend[pl.ds(0, n_sim, stride=8), :] = jnp.where(left16, g[0:16, :], g[16:32, :])
    gsend[pl.ds(1, n_sim, stride=8), :] = jnp.where(left16, g[32:48, :], g[48:64, :])
    for k in range(1, n_sim):
        to = sim_peer(k)
        pltpu.make_async_remote_copy(
            gsend.at[block(to), :], grecv.at[block(me), :], send_sem.at[4], g_sem,
            device_id=(sec, to), device_id_type=MESH,
        ).start()
    grecv[block(me), :] = gsend[block(me), :]

    arrived(zrecv, 16 * (n_sim - 1), z_sem)
    part, all_mean, all_count = merged(zrecv, n_sim)
    frecv[block(sec), :] = part
    for k in range(1, n_sec):
        pltpu.make_async_remote_copy(
            frecv.at[block(sec), :], frecv.at[block(sec), :], send_sem.at[5], f_sem,
            device_id=(sec_peer(k), me), device_id_type=MESH,
        ).start()
    gmean_out[...] = all_mean[:, 0:width]

    corrb[...] = co / (n64[...] - 1.0)
    for pp in range(2):
        for rr in range(2):
            a = corrb[pl.ds(4 * rr + pp, half, stride=8), :]
            b = corrb[pl.ds(4 * rr + 2 + pp, half, stride=8), :]
            turned = turn if rr == 0 else turn2
            turned[pl.ds(pairs * pp, half, stride=2), :] = jnp.where(left8, a, pltpu.roll(b, width, 1))
            turned[pl.ds(pairs * pp + 1, half, stride=2), :] = jnp.where(left8, pltpu.roll(a, width, 1), b)
    cov_out[:, 0:128] = turn[...]
    cov_out[:, 128:256] = turn2[...]

    arrived(grecv, 8 * (n_sim - 1), g_sem)
    grp[pl.ds(0, n_sim, stride=2), :] = grecv[pl.ds(0, n_sim, stride=8), :]
    grp[pl.ds(1, n_sim, stride=2), :] = grecv[pl.ds(1, n_sim, stride=8), :]
    grp_out[...] = (grp[...] + between) / jnp.maximum(grp_count - 1.0, 1.0)

    arrived(frecv, 8 * (n_sec - 1), f_sem)
    gcov_out[...] = (frecv[...] / (all_count - 1.0))[:, 0:width]

    arrived(sums, n_sim - 1, send_sem.at[0])
    arrived(recvb, n_sim - 1, send_sem.at[1])
    arrived(qrecv, 16 * (n_sec - 1), send_sem.at[2])
    arrived(zrecv, 16 * (n_sim - 1), send_sem.at[3])
    arrived(grecv, 8 * (n_sim - 1), send_sem.at[4])
    arrived(frecv, 8 * (n_sec - 1), send_sem.at[5])


def put(n, *refs):
    ins, outs, sem = refs[:n], refs[n:2 * n], refs[2 * n]
    copies = [pltpu.make_async_copy(a, b, sem.at[i]) for i, (a, b) in enumerate(zip(ins, outs))]
    for c in copies:
        c.start()
    for c in copies:
        c.wait()


def solution(mesh):
    n_sec, n_sim = mesh.shape["section"], mesh.shape["sim"]
    chunks = 4

    def local(state, owner, counts):
        slabs, width, cells = state.shape
        pairs = slabs // 2
        half = pairs // 2
        vmem = pl.BlockSpec(memory_space=pltpu.VMEM)
        smem = pl.BlockSpec(memory_space=pltpu.SMEM)
        dma = pltpu.SemaphoreType.DMA
        hbm = pl.BlockSpec(memory_space=pltpu.HBM)
        shapes = [
            jax.ShapeDtypeStruct((slabs, width), F32),
            jax.ShapeDtypeStruct((slabs, width * width // n_sim), F32),
            jax.ShapeDtypeStruct((width // 2, 2 * width), F32),
            jax.ShapeDtypeStruct((1, width), F32),
            jax.ShapeDtypeStruct((width, width), F32),
        ]
        found = pl.pallas_call(
            functools.partial(kernel, n_sec, n_sim, width, chunks),
            out_shape=shapes,
            in_specs=[hbm] * 3,
            out_specs=[vmem] * 5,
            scratch_shapes=[
                pltpu.VMEM((pairs, 2 * width, cells), F32),
                pltpu.VMEM((2, 2, 4 * width, cells), BF16),
                pltpu.VMEM((128, 128), F32),
                pltpu.VMEM((n_sim, pairs, 128), F32),
                pltpu.VMEM((half, 2 * width, 128), F32),
                pltpu.VMEM((n_sim, half, 8, 128), F32),
                pltpu.VMEM((16 * n_sec, 128), F32),
                pltpu.VMEM((16 * n_sec, 128), F32),
                pltpu.VMEM((16 * n_sim, 128), F32),
                pltpu.VMEM((8 * n_sec, 128), F32),
                pltpu.VMEM((8 * n_sim, 128), F32),
                pltpu.VMEM((8 * n_sim, 128), F32),
                pltpu.VMEM((width // 2, 128), F32),
                pltpu.VMEM((width, 128), F32),
                pltpu.VMEM((width, 128), F32),
                pltpu.VMEM((width, 128), jnp.int32),
                pltpu.VMEM((slabs, 128), F32),
                pltpu.VMEM((slabs, 128), F32),
                pltpu.SMEM((slabs,), jnp.int32),
                pltpu.SMEM((slabs,), jnp.int32),
                dma((pairs,)),
                dma((2,)),
                dma((6,)),
                dma(()),
                dma((chunks,)),
                dma(()),
                dma(()),
                dma(()),
                dma(()),
            ],
            compiler_params=pltpu.CompilerParams(
                collective_id=0, has_side_effects=True, vmem_limit_bytes=32 * 1024 * 1024
            ),
            name="moments",
        )(*(
            pltpu.with_memory_space_constraint(a, pltpu.HBM)
            for a in (state.reshape(pairs, 2 * width, cells), counts, owner.reshape(slabs))
        ))
        mean, cov, grp, gmean, gcov = pl.pallas_call(
            functools.partial(put, 5),
            out_shape=shapes,
            in_specs=[vmem] * 5,
            out_specs=[hbm] * 5,
            scratch_shapes=[dma((5,))],
            compiler_params=pltpu.CompilerParams(vmem_limit_bytes=4 * 1024 * 1024),
            name="put",
        )(*found)
        return mean, cov, grp.reshape(1, width * width), gmean.reshape(width), gcov

    return jax.shard_map(
        local,
        mesh=mesh,
        in_specs=(P("section", None, "sim"), P("section", None), P("section")),
        out_specs=(P("section", None), P("section", "sim"), P(("section", "sim"), None), P(), P()),
        check_vma=False,
    )
```

time: 31.4 us -> 27.1 us (0.86)
  Pallas kernels: 30.7 us -> 26.4 us
    pallas_call x1, Pallas kernels: 30 us -> 25.7 us  [local(): pl.pallas_call(functools.partial(kernel, n_sec, n_sim, width, chunks), ou...]
where the time goes in v3:
time: 27.1 us; the launch traced here: 27 us
  Pallas kernels  26.4 us (97%)
  between operations  0.64 us (2%)
    pallas_call x1, Pallas kernels, local(): pl.pallas_call(functools.partial(kernel, n_sec, n_sim, width, chunks), ou...  25.7 us
    pallas_call x1, Pallas kernels, local(): pl.pallas_call(functools.partial(put, 5), out_shape=shapes, in_specs=[vme...  0.69 us

profile of v3, /device:TPU:1, one launch (start us, length us, event | category | flops | bytes accessed | tf_op | source)
XLA Modules:
  0.0 27.0 jit_solution(2992305798135144326)
XLA Ops:
  0.6 25.7 %moments.1 = (f32[32,64]{1,0:T(8,128)S(1)}, f32[32,256]{1,0:T(8,128)S(1)}, f32[32,128]{1,0:T(8,128)S(1)}, f32[1,64]{1,0:T(1,128)S(1)}, f32[64,64]{1,0:T(8,128)S(1)}) custom-call(f32[16,128,1024]{2,1,0:T(8,128)} %bitcast.4, s32[32]{0:T(128)} %counts_hbm.1, s32[32]{0:T(128)} %bitcast.5), custom_call_target="tpu_custom_call" | custom-call | tf_op jit(solution)/shard_map/moments/pallas_call | solution.py:335
  26.3 0.7 %put.1 = (f32[32,64]{1,0:T(8,128)}, f32[32,256]{1,0:T(8,128)}, f32[32,128]{1,0:T(8,128)}, f32[1,64]{1,0:T(1,128)}, f32[64,64]{1,0:T(8,128)}) custom-call(f32[32,64]{1,0:T(8,128)S(1)} %get-tuple-element.15.refs_0_, f32[32,256]{1,0:T(8,128)S(1)} %get-tuple-element.16.refs_1_, f32[32,128]{1,0:T(8,128)S(1)} %get-tuple-element.17.refs_2_, ...), custom_call_target="tpu_custom_call" | custom-call | tf_op jit(solution)/shard_map/put/pallas_call | solution.py:379

commit v4 on v3

--- a/solution.py
+++ b/solution.py
@@ -8,7 +8,6 @@
 from jax.sharding import PartitionSpec as P
 
 MESH = pl.DeviceIdType.MESH
-HIGH = lax.Precision.HIGHEST
 F32 = jnp.float32
 BF16 = jnp.bfloat16
 
@@ -17,8 +16,11 @@
     return lax.dot_general(a, b, (((1,), (1,)), ((), ())), preferred_element_type=F32)
 
 
-def dot_high(a, b):
-    return jnp.dot(a, b, precision=HIGH, preferred_element_type=F32)
+def outer_sum(a, b):
+    a_top, b_top = a.astype(BF16).astype(F32), b.astype(BF16).astype(F32)
+    left = jnp.concatenate([a_top, a - a_top, a_top], axis=0)
+    right = jnp.concatenate([b_top, b_top, b - b_top], axis=0)
+    return jnp.dot(left.T.astype(BF16), right.astype(BF16), preferred_element_type=F32)
 
 
 def iota(shape, dim):
@@ -26,11 +28,11 @@
 
 
 def kernel(
-    n_sec, n_sim, width, chunks,
+    n_sec, n_sim, width,
     state, counts_hbm, owner_hbm,
     mean_out, cov_out, grp_out, gmean_out, gcov_out,
-    xv, split, colsum, sums, sendb, recvb, qbuf, qrecv, zrecv, frecv, gsend, grecv, grp, corrb, n64, own64, turn, turn2,
-    counts, owner, load_sem, int_sem, send_sem, sums_sem, piece_sem, q_sem, z_sem, f_sem, g_sem,
+    xv, split, colsum, sums, sendb, first_x, first_z, part_x, part_z, second_x, second_z, straight, sel, gaps, fold, qrecv, zrecv, gsend, grecv, grp, corrb, n64, own64, turn, turn2,
+    counts, owner, load_sem, int_sem, send_sem, sums_sem, first_sem, second_sem, straight_sem, q_sem, z_sem, g_sem,
 ):
     pairs, _, cells = xv.shape
     half = pairs // 2
@@ -48,8 +50,11 @@
     def block(i):
         return pl.ds(pl.multiple_of(8 * i, 8), 8)
 
-    def double(i):
-        return pl.ds(pl.multiple_of(16 * i, 16), 16)
+    def along_x(k):
+        return (x + k) % 4
+
+    def along_z(k):
+        return (z + k) % 4
 
     def arrived(ref, n, sem):
         pltpu.make_async_copy(ref.at[pl.ds(0, n)], ref.at[pl.ds(0, n)], sem).wait()
@@ -97,6 +102,11 @@
         o_odd = jnp.where(here, owner[2 * p + 1], o_odd)
     n_int = jnp.where(left16, c_even, c_odd)
     colsum[...] = jnp.zeros((128, 128), F32)
+    row128, col128 = iota((128, 128), 0), iota((128, 128), 1)
+    for r in range(4):
+        sel[:, 128 * r:128 * (r + 1)] = jnp.where(
+            row128 == (col128 // width) * width + 4 * me + r, 1.0, 0.0
+        ).astype(BF16)
     gsend[...] = jnp.zeros((8 * n_sim, 128), F32)
 
     lane_c = iota((1, cells), 1)
@@ -111,44 +121,58 @@
             for h in range(2):
                 n = jnp.clip(counts[2 * p + h] - base, 0, cells)
                 live = lane_c < n
-                cell = xv[p, h * width:(h + 1) * width, :]
-                s = jnp.sum(jnp.where(live, cell, 0.0), axis=1, keepdims=True)
-                colsum[h * width:(h + 1) * width, p:p + 1] = s
-                m = s / jnp.maximum(n, 1).astype(F32)
-                c = jnp.where(live, cell - m, 0.0)
-                top = c.astype(BF16)
-                split[i % 2, pp, h * width:(h + 1) * width, :] = top
-                split[i % 2, pp, (2 + h) * width:(3 + h) * width, :] = (c - top.astype(F32)).astype(BF16)
+                for r in range(h * width, (h + 1) * width, 16):
+                    cell = xv[p, r:r + 16, :]
+                    s = jnp.sum(jnp.where(live, cell, 0.0), axis=1, keepdims=True)
+                    colsum[r:r + 16, p:p + 1] = s
+                    m = s / jnp.maximum(n, 1).astype(F32)
+                    c = jnp.where(live, cell - m, 0.0)
+                    top = c.astype(BF16)
+                    split[i % 2, pp, r:r + 16, :] = top
+                    split[i % 2, pp, 2 * width + r:2 * width + r + 16, :] = (c - top.astype(F32)).astype(BF16)
 
     def multiply(i, qsum):
         for pp in range(2):
-            both = dot_rows(split[i % 2, pp, 0:2 * width, :], split[i % 2, pp])
-            cross = both[:, 128:256]
-            full = both[:, 0:128] + cross + cross.T
+            both = dot_rows(split[i % 2, pp], split[i % 2, pp, 0:2 * width, :])
+            cross = both[2 * width:, :]
+            full = both[0:2 * width, :] + cross + cross.T
             co = jnp.where(left64, full[0:width, :], full[width:, :])
             qsum = qsum + co
-            sendb[i, pl.ds(pp, width, stride=2), :] = co
+            for j in range(4):
+                sendb[i, j, pl.ds(pp, width // 4, stride=2), :] = co[width // 4 * j:width // 4 * (j + 1), :]
         return qsum
 
-    per = half // chunks
+    staged = first_x.shape[1]
     qsum = jnp.zeros((width, 128), F32)
     for i in range(half + 1):
         if i < half:
             centre(i)
         if i > 0:
             qsum = multiply(i - 1, qsum)
-        if i > 0 and i % per == 0:
-            t = i // per - 1
+        if i > 0 and i % 2 == 0:
+            t = i // 2 - 1
             if t == 0:
                 pl.semaphore_wait(barrier, n_sim - 1 + n_sec - 1)
-            for k in range(1, n_sim):
-                to = sim_peer(k)
-                pltpu.make_async_remote_copy(
-                    sendb.at[pl.ds(t * per, per), block(to), :],
-                    recvb.at[me, pl.ds(t * per, per)],
-                    send_sem.at[1], piece_sem.at[t],
-                    device_id=(sec, to), device_id_type=MESH,
-                ).start()
+            if t < staged:
+                for k in range(1, 4):
+                    to = along_x(k)
+                    pltpu.make_async_remote_copy(
+                        sendb.at[i - 2, :, block(to), :], first_x.at[k - 1, t], send_sem.at[1], first_sem.at[t, 0],
+                        device_id=(sec, z * 4 + to), device_id_type=MESH,
+                    ).start()
+                    to = along_z(k)
+                    pltpu.make_async_remote_copy(
+                        sendb.at[i - 1, to], first_z.at[k - 1, t], send_sem.at[7], first_sem.at[t, 1],
+                        device_id=(sec, to * 4 + x), device_id_type=MESH,
+                    ).start()
+            else:
+                for k in range(1, n_sim):
+                    pltpu.make_async_remote_copy(
+                        sendb.at[pl.ds(i - 2, 2), along_z(k // 4), block(along_x(k % 4)), :],
+                        straight.at[k - 1, t - staged],
+                        send_sem.at[5], straight_sem.at[t - staged],
+                        device_id=(sec, sim_peer(k)), device_id_type=MESH,
+                    ).start()
     mine = colsum[...].T[0:pairs, :]
     sums[me] = mine
     for k in range(1, n_sim):
@@ -156,7 +180,6 @@
             sums.at[me], sums.at[me], send_sem.at[0], sums_sem,
             device_id=(sec, sim_peer(k)), device_id_type=MESH,
         ).start()
-    recvb[me] = sendb[:, block(me), :]
 
     def both_sides(value):
         turned = pltpu.roll(value, width, 1)
@@ -168,7 +191,7 @@
         d_even, d_odd = m_even - mean, m_odd - mean
         off = jnp.concatenate([d_even, d_odd], axis=0)
         left = jnp.concatenate([w_even * d_even, w_odd * d_odd], axis=0)
-        return count, mean, dot_high(left.T, off)[0:width, :]
+        return count, mean, outer_sum(left, off)[0:width, :]
 
     def here(c, d):
         return jnp.clip(c - d * cells, 0, cells).astype(F32)
@@ -177,44 +200,90 @@
     l_even, l_odd = both_sides(mine / jnp.maximum(n_mine, 1.0))
     dev_count, dev_mean, dev_co = about(l_even, l_odd, here(c_even, me), here(c_odd, me))
     q = qsum + pltpu.roll(qsum, width, 1) + dev_co
-    rows8 = jnp.where(sub8 == 0, dev_mean, jnp.where(sub8 == 1, dev_count, 0.0))
-    for s in range(n_sec):
-        qbuf[16 * s:16 * s + 8, :] = q[8 * s:8 * s + 8, :]
-        qbuf[16 * s + 8:16 * s + 16, :] = rows8
+
+    lane32, sub32 = iota((width // 2, 128), 1), iota((width // 2, 128), 0)
+    left32 = lane32 < width
+    col32 = lane32 % width
+    inner32 = col32 < width // 2
+    above32 = col32 > sub32
+
+    def folded(m, mean, count):
+        top, bottom = m[0:width // 2, :], m[width // 2:width, :]
+        kept = jnp.where(inner32 & ~above32, pltpu.roll(bottom, width // 2, 1), top)
+        diagonal = jnp.sum(jnp.where(col32 == sub32, top, 0.0), axis=0, keepdims=True)
+        info = jnp.where(sub8 == 0, mean, jnp.where(sub8 == 1, count, jnp.where(sub8 == 2, diagonal, 0.0)))
+        quarter = width // 4
+        return jnp.concatenate(
+            [jnp.where(left16, kept[0:quarter, :], kept[quarter:2 * quarter, :]), info], axis=0
+        )
+
+    def unfolded(m):
+        swapped = pltpu.roll(m[0:pairs, :], width, 1)
+        kept = jnp.concatenate(
+            [jnp.where(left16, m[0:pairs, :], swapped), jnp.where(left16, swapped, m[0:pairs, :])], axis=0
+        )
+        turned = jnp.concatenate([kept, kept, kept, kept], axis=0).T[0:width, :]
+        first = jnp.where(above32, kept, jnp.where(col32 == sub32, m[pairs + 2:pairs + 3, :], turned[0:width // 2, :]))
+        top = jnp.where(inner32, first, kept)
+        last = pltpu.roll(jnp.where(above32, turned[0:width // 2, :], kept), width // 2, 1)
+        bottom = jnp.where(inner32, turned[width // 2:, :], last)
+        return jnp.concatenate([top, bottom], axis=0)
+
+    def third(i):
+        return pl.ds(pl.multiple_of(24 * i, 8), 24)
+
+    fold[...] = folded(q, dev_mean, dev_count)
     for k in range(1, n_sec):
-        to = sec_peer(k)
-        pltpu.make_async_remote_copy(
-            qbuf.at[double(to), :], qrecv.at[double(sec), :], send_sem.at[2], q_sem,
-            device_id=(to, me), device_id_type=MESH,
-        ).start()
-    qrecv[double(sec), :] = qbuf[double(sec), :]
+        pltpu.make_async_remote_copy(
+            fold, qrecv.at[third(sec), :], send_sem.at[2], q_sem,
+            device_id=(sec_peer(k), me), device_id_type=MESH,
+        ).start()
+    qrecv[third(sec), :] = fold[...]
 
     lane64, sub64 = iota((width, 128), 1), iota((width, 128), 0)
     names = jnp.where(
         ((sub64 % 8) // 2 == (lane64 % width) // n_sim) & (own64[...] == lane64 % n_sim), 1.0, 0.0
-    ).T
+    )
+    names = jnp.concatenate([names, names], axis=0).T.astype(BF16)
 
     def merged(ref, n):
-        part = ref[0:8, :]
+        part = ref[0:24, :]
         for s in range(1, n):
-            part = part + ref[16 * s:16 * s + 8, :]
-        means = ref[pl.ds(8, n, stride=16), :]
-        weights = ref[pl.ds(9, n, stride=16), :]
+            part = part + ref[24 * s:24 * (s + 1), :]
+        means = ref[pl.ds(pairs, n, stride=24), :]
+        weights = ref[pl.ds(pairs + 1, n, stride=24), :]
         count = jnp.sum(weights, axis=0, keepdims=True)
         mean = jnp.sum(weights * means, axis=0, keepdims=True) / jnp.maximum(count, 1.0)
         gap = means - mean
-        corrb[...] = dot_high((weights * gap).T, gap)[0:width, :]
-        return part + corrb[block(sec), :], mean, count
-
-    arrived(qrecv, 16 * (n_sec - 1), q_sem)
-    part, part_mean, part_count = merged(qrecv, n_sec)
-    own_z = double(me)
-    zrecv[own_z, :] = jnp.concatenate(
-        [part, jnp.where(sub8 == 0, part_mean, jnp.where(sub8 == 1, part_count, 0.0))], axis=0
-    )
+        return part, mean, count, outer_sum(weights * gap, gap)[0:width, :]
+
+    for t in range(staged):
+        few = first_x.at[:, t]
+        pltpu.make_async_copy(few, few, first_sem.at[t, 0]).wait()
+        few = first_z.at[:, t]
+        pltpu.make_async_copy(few, few, first_sem.at[t, 1]).wait()
+        part_x[t] = sendb[2 * t, :, block(x), :] + first_x[0, t] + first_x[1, t] + first_x[2, t]
+        part_z[t] = sendb[2 * t + 1, z] + first_z[0, t] + first_z[1, t] + first_z[2, t]
+    for k in range(1, 4):
+        to = along_z(k)
+        pltpu.make_async_remote_copy(
+            part_x.at[:, to], second_x.at[k - 1], send_sem.at[6], second_sem.at[0],
+            device_id=(sec, to * 4 + x), device_id_type=MESH,
+        ).start()
+        to = along_x(k)
+        pltpu.make_async_remote_copy(
+            part_z.at[:, block(to), :], second_z.at[k - 1], send_sem.at[8], second_sem.at[1],
+            device_id=(sec, z * 4 + to), device_id_type=MESH,
+        ).start()
+
+    arrived(qrecv, 24 * (n_sec - 1), q_sem)
+    part, part_mean, part_count, part_co = merged(qrecv, n_sec)
+    extra = folded(part_co, part_mean, part_count)
+    info = jnp.where(sub8 == 2, part[pairs:, :] + extra[pairs:, :], extra[pairs:, :])
+    zrecv[third(me), :] = jnp.concatenate([part[0:pairs, :] + extra[0:pairs, :], info], axis=0)
     for k in range(1, n_sim):
         pltpu.make_async_remote_copy(
-            zrecv.at[own_z, :], zrecv.at[own_z, :], send_sem.at[3], z_sem,
+            zrecv.at[third(me), :], zrecv.at[third(me), :], send_sem.at[3], z_sem,
             device_id=(sec, sim_peer(k)), device_id_type=MESH,
         ).start()
 
@@ -227,18 +296,22 @@
     turn[pl.ds(1, pairs, stride=2), :] = pltpu.roll(means, width, 1)
     mean_out[...] = turn[:, 0:width]
 
-    rows = [jnp.zeros((pairs, 128), F32) for _ in range(4)]
-    to_front = (128 - 4 * me) % 128
+    weighted = []
     for d in range(n_sim):
         n = here(n_int, d)
         gap = sums[d] / jnp.maximum(n, 1.0) - means
-        front = pltpu.roll(gap, to_front, 1)
-        gap_n = gap * n
-        for r in range(4):
-            rows[r] = rows[r] + jnp.where(left16, front[:, r:r + 1], front[:, width + r:width + r + 1]) * gap_n
+        weighted.append(gap * n)
+        top = gap.astype(BF16)
+        gaps[pairs * d:pairs * (d + 1), :] = top
+        gaps[pairs * (n_sim + d):pairs * (n_sim + d + 1), :] = (gap - top.astype(F32)).astype(BF16)
     for r in range(4):
+        picked = jnp.dot(gaps[...], sel[:, 128 * r:128 * (r + 1)], preferred_element_type=F32)
+        rows = jnp.zeros((pairs, 128), F32)
+        for d in range(n_sim):
+            one = picked[pairs * d:pairs * (d + 1), :] + picked[pairs * (n_sim + d):pairs * (n_sim + d + 1), :]
+            rows = rows + one * weighted[d]
         for pp in range(2):
-            corrb[pl.ds(2 * r + pp, half, stride=8), :] = rows[r][half * pp:half * (pp + 1), :]
+            corrb[pl.ds(2 * r + pp, half, stride=8), :] = rows[half * pp:half * (pp + 1), :]
     co = corrb[...]
     m_even, m_odd = both_sides(means)
     grp_count, _, grp_co = about(
@@ -246,15 +319,26 @@
         jnp.where(o_even == me, c_even, 0).astype(F32), jnp.where(o_odd == me, c_odd, 0).astype(F32),
     )
     corrb[...] = grp_co
-    left32 = iota((width // 2, 128), 1) < width
     between = jnp.where(left32, corrb[pl.ds(0, width // 2, stride=2), :], corrb[pl.ds(1, width // 2, stride=2), :])
 
-    for t in range(chunks):
-        few = recvb.at[pl.ds(0, n_sim - 1), pl.ds(0, per)]
-        pltpu.make_async_copy(few, few, piece_sem.at[t]).wait()
-    for d in range(n_sim):
-        co = co + recvb[d].reshape(width, 128)
-    named = dot_high(names, co)
+    pltpu.make_async_copy(second_x, second_x, second_sem.at[0]).wait()
+    pltpu.make_async_copy(second_z, second_z, second_sem.at[1]).wait()
+    tiles = []
+    for t in range(staged):
+        tiles.append(part_x[t, z] + second_x[0, t] + second_x[1, t] + second_x[2, t])
+        tiles.append(part_z[t, block(x), :] + second_z[0, t] + second_z[1, t] + second_z[2, t])
+    for t in range(half // 2 - staged):
+        few = straight.at[:, t]
+        pltpu.make_async_copy(few, few, straight_sem.at[t]).wait()
+        for u in range(2):
+            tile = sendb[2 * (staged + t) + u, z, block(x), :]
+            for k in range(n_sim - 1):
+                tile = tile + straight[k, t, u]
+            tiles.append(tile)
+    co = co + jnp.concatenate(tiles, axis=0)
+    top = co.astype(BF16)
+    low = (co - top.astype(F32)).astype(BF16)
+    named = jnp.dot(names, jnp.concatenate([top, low], axis=0), preferred_element_type=F32)
     g = jnp.where(left64, named[0:width, :], named[width:, :])
     g = g + pltpu.roll(g, width, 1)
     gsend[pl.ds(0, n_sim, stride=8), :] = jnp.where(left16, g[0:16, :], g[16:32, :])
@@ -267,15 +351,10 @@
         ).start()
     grecv[block(me), :] = gsend[block(me), :]
 
-    arrived(zrecv, 16 * (n_sim - 1), z_sem)
-    part, all_mean, all_count = merged(zrecv, n_sim)
-    frecv[block(sec), :] = part
-    for k in range(1, n_sec):
-        pltpu.make_async_remote_copy(
-            frecv.at[block(sec), :], frecv.at[block(sec), :], send_sem.at[5], f_sem,
-            device_id=(sec_peer(k), me), device_id_type=MESH,
-        ).start()
+    arrived(zrecv, 24 * (n_sim - 1), z_sem)
+    part, all_mean, all_count, all_co = merged(zrecv, n_sim)
     gmean_out[...] = all_mean[:, 0:width]
+    gcov_out[...] = ((unfolded(part) + all_co) / (all_count - 1.0))[:, 0:width]
 
     corrb[...] = co / (n64[...] - 1.0)
     for pp in range(2):
@@ -293,15 +372,15 @@
     grp[pl.ds(1, n_sim, stride=2), :] = grecv[pl.ds(1, n_sim, stride=8), :]
     grp_out[...] = (grp[...] + between) / jnp.maximum(grp_count - 1.0, 1.0)
 
-    arrived(frecv, 8 * (n_sec - 1), f_sem)
-    gcov_out[...] = (frecv[...] / (all_count - 1.0))[:, 0:width]
-
     arrived(sums, n_sim - 1, send_sem.at[0])
-    arrived(recvb, n_sim - 1, send_sem.at[1])
-    arrived(qrecv, 16 * (n_sec - 1), send_sem.at[2])
-    arrived(zrecv, 16 * (n_sim - 1), send_sem.at[3])
+    arrived(first_x, 3, send_sem.at[1])
+    arrived(first_z, 3, send_sem.at[7])
+    arrived(qrecv, 24 * (n_sec - 1), send_sem.at[2])
+    arrived(zrecv, 24 * (n_sim - 1), send_sem.at[3])
     arrived(grecv, 8 * (n_sim - 1), send_sem.at[4])
-    arrived(frecv, 8 * (n_sec - 1), send_sem.at[5])
+    arrived(straight, n_sim - 1, send_sem.at[5])
+    arrived(second_x, 3, send_sem.at[6])
+    arrived(second_z, 3, send_sem.at[8])
 
 
 def put(n, *refs):
@@ -315,12 +394,12 @@
 
 def solution(mesh):
     n_sec, n_sim = mesh.shape["section"], mesh.shape["sim"]
-    chunks = 4
 
     def local(state, owner, counts):
         slabs, width, cells = state.shape
         pairs = slabs // 2
         half = pairs // 2
+        staged = 2
         vmem = pl.BlockSpec(memory_space=pltpu.VMEM)
         smem = pl.BlockSpec(memory_space=pltpu.SMEM)
         dma = pltpu.SemaphoreType.DMA
@@ -333,7 +412,7 @@
             jax.ShapeDtypeStruct((width, width), F32),
         ]
         found = pl.pallas_call(
-            functools.partial(kernel, n_sec, n_sim, width, chunks),
+            functools.partial(kernel, n_sec, n_sim, width),
             out_shape=shapes,
             in_specs=[hbm] * 3,
             out_specs=[vmem] * 5,
@@ -342,12 +421,19 @@
                 pltpu.VMEM((2, 2, 4 * width, cells), BF16),
                 pltpu.VMEM((128, 128), F32),
                 pltpu.VMEM((n_sim, pairs, 128), F32),
-                pltpu.VMEM((half, 2 * width, 128), F32),
-                pltpu.VMEM((n_sim, half, 8, 128), F32),
-                pltpu.VMEM((16 * n_sec, 128), F32),
-                pltpu.VMEM((16 * n_sec, 128), F32),
-                pltpu.VMEM((16 * n_sim, 128), F32),
-                pltpu.VMEM((8 * n_sec, 128), F32),
+                pltpu.VMEM((half, 4, 32, 128), F32),
+                pltpu.VMEM((3, staged, 4, 8, 128), F32),
+                pltpu.VMEM((3, staged, 32, 128), F32),
+                pltpu.VMEM((staged, 4, 8, 128), F32),
+                pltpu.VMEM((staged, 32, 128), F32),
+                pltpu.VMEM((3, staged, 8, 128), F32),
+                pltpu.VMEM((3, staged, 8, 128), F32),
+                pltpu.VMEM((n_sim - 1, half // 2 - staged, 2, 8, 128), F32),
+                pltpu.VMEM((128, 512), BF16),
+                pltpu.VMEM((2 * n_sim * pairs, 128), BF16),
+                pltpu.VMEM((24, 128), F32),
+                pltpu.VMEM((24 * n_sec, 128), F32),
+                pltpu.VMEM((24 * n_sim, 128), F32),
                 pltpu.VMEM((8 * n_sim, 128), F32),
                 pltpu.VMEM((8 * n_sim, 128), F32),
                 pltpu.VMEM((width // 2, 128), F32),
@@ -360,10 +446,11 @@
                 pltpu.SMEM((slabs,), jnp.int32),
                 dma((pairs,)),
                 dma((2,)),
-                dma((6,)),
+                dma((9,)),
                 dma(()),
-                dma((chunks,)),
-                dma(()),
+                dma((staged, 2)),
+                dma((2,)),
+                dma((half // 2 - staged,)),
                 dma(()),
                 dma(()),
                 dma(()),

time: 27.1 us -> 24.3 us (0.90)
  Pallas kernels: 26.4 us -> 23.5 us
    pallas_call x1, Pallas kernels: 25.7 us -> 22.9 us  [local(): pl.pallas_call(functools.partial(kernel, n_sec, n_sim, width), out_shape=...]
where the time goes in v4:
time: 24.3 us; the launch traced here: 24.2 us
  Pallas kernels  23.5 us (97%)
  between operations  0.64 us (3%)
    pallas_call x1, Pallas kernels, local(): pl.pallas_call(functools.partial(kernel, n_sec, n_sim, width), out_shape=...  22.9 us
    pallas_call x1, Pallas kernels, local(): pl.pallas_call(functools.partial(put, 5), out_shape=shapes, in_specs=[vme...  0.69 us

profile of v4, /device:TPU:1, one launch (start us, length us, event | category | flops | bytes accessed | tf_op | source)
XLA Modules:
  0.0 24.2 jit_solution(16903967775442890497)
XLA Ops:
  0.6 22.9 %moments.1 = (f32[32,64]{1,0:T(8,128)S(1)}, f32[32,256]{1,0:T(8,128)S(1)}, f32[32,128]{1,0:T(8,128)S(1)}, f32[1,64]{1,0:T(1,128)S(1)}, f32[64,64]{1,0:T(8,128)S(1)}) custom-call(f32[16,128,1024]{2,1,0:T(8,128)} %bitcast.4, s32[32]{0:T(128)} %counts_hbm.1, s32[32]{0:T(128)} %bitcast.5), custom_call_target="tpu_custom_call" | custom-call | tf_op jit(solution)/shard_map/moments/pallas_call | solution.py:414
  23.5 0.7 %put.1 = (f32[32,64]{1,0:T(8,128)}, f32[32,256]{1,0:T(8,128)}, f32[32,128]{1,0:T(8,128)}, f32[1,64]{1,0:T(1,128)}, f32[64,64]{1,0:T(8,128)}) custom-call(f32[32,64]{1,0:T(8,128)S(1)} %get-tuple-element.15.refs_0_, f32[32,256]{1,0:T(8,128)S(1)} %get-tuple-element.16.refs_1_, f32[32,128]{1,0:T(8,128)S(1)} %get-tuple-element.17.refs_2_, ...), custom_call_target="tpu_custom_call" | custom-call | tf_op jit(solution)/shard_map/put/pallas_call | solution.py:466

commit v5 on v4

--- a/solution.py
+++ b/solution.py
@@ -115,9 +115,6 @@
     def centre(i):
         for pp in range(2):
             p = i + half * pp
-            loads[p].wait()
-        for pp in range(2):
-            p = i + half * pp
             for h in range(2):
                 n = jnp.clip(counts[2 * p + h] - base, 0, cells)
                 live = lane_c < n
@@ -133,9 +130,10 @@
 
     def multiply(i, qsum):
         for pp in range(2):
-            both = dot_rows(split[i % 2, pp], split[i % 2, pp, 0:2 * width, :])
-            cross = both[2 * width:, :]
-            full = both[0:2 * width, :] + cross + cross.T
+            terms = split[i % 2, pp]
+            both = dot_rows(terms, terms)
+            full = both[0:2 * width, :] + both[2 * width:, :]
+            full = full[:, 0:2 * width] + full[:, 2 * width:]
             co = jnp.where(left64, full[0:width, :], full[width:, :])
             qsum = qsum + co
             for j in range(4):
@@ -145,10 +143,22 @@
     staged = first_x.shape[1]
     qsum = jnp.zeros((width, 128), F32)
     for i in range(half + 1):
+        if i == 0 or i % 2 == 1:
+            for p in range(i, min(half, i + 1 + i % 2)):
+                loads[p].wait()
+                loads[p + half].wait()
         if i < half:
             centre(i)
         if i > 0:
             qsum = multiply(i - 1, qsum)
+        if i == half - 1:
+            mine = colsum[...].T[0:pairs, :]
+            sums[me] = mine
+            for k in range(1, n_sim):
+                pltpu.make_async_remote_copy(
+                    sums.at[me], sums.at[me], send_sem.at[0], sums_sem,
+                    device_id=(sec, sim_peer(k)), device_id_type=MESH,
+                ).start()
         if i > 0 and i % 2 == 0:
             t = i // 2 - 1
             if t == 0:
@@ -173,14 +183,6 @@
                         send_sem.at[5], straight_sem.at[t - staged],
                         device_id=(sec, sim_peer(k)), device_id_type=MESH,
                     ).start()
-    mine = colsum[...].T[0:pairs, :]
-    sums[me] = mine
-    for k in range(1, n_sim):
-        pltpu.make_async_remote_copy(
-            sums.at[me], sums.at[me], send_sem.at[0], sums_sem,
-            device_id=(sec, sim_peer(k)), device_id_type=MESH,
-        ).start()
-
     def both_sides(value):
         turned = pltpu.roll(value, width, 1)
         return jnp.where(left16, value, turned), jnp.where(left16, turned, value)

time: 24.3 us -> 23.5 us (0.967)
  Pallas kernels: 23.5 us -> 22.7 us
    pallas_call x1, Pallas kernels: 22.9 us -> 22 us  [local(): pl.pallas_call(functools.partial(kernel, n_sec, n_sim, width), out_shape=...]
where the time goes in v5:
time: 23.5 us; the launch traced here: 23.3 us
  Pallas kernels  22.7 us (97%)
  between operations  0.64 us (3%)
    pallas_call x1, Pallas kernels, local(): pl.pallas_call(functools.partial(kernel, n_sec, n_sim, width), out_shape=...  22 us
    pallas_call x1, Pallas kernels, local(): pl.pallas_call(functools.partial(put, 5), out_shape=shapes, in_specs=[vme...  0.69 us

profile of v5, /device:TPU:1, one launch (start us, length us, event | category | flops | bytes accessed | tf_op | source)
XLA Modules:
  0.0 23.3 jit_solution(2901612396087046040)
XLA Ops:
  0.6 22.0 %moments.1 = (f32[32,64]{1,0:T(8,128)S(1)}, f32[32,256]{1,0:T(8,128)S(1)}, f32[32,128]{1,0:T(8,128)S(1)}, f32[1,64]{1,0:T(1,128)S(1)}, f32[64,64]{1,0:T(8,128)S(1)}) custom-call(f32[16,128,1024]{2,1,0:T(8,128)} %bitcast.4, s32[32]{0:T(128)} %counts_hbm.1, s32[32]{0:T(128)} %bitcast.5), custom_call_target="tpu_custom_call" | custom-call | tf_op jit(solution)/shard_map/moments/pallas_call | solution.py:416
  22.7 0.7 %put.1 = (f32[32,64]{1,0:T(8,128)}, f32[32,256]{1,0:T(8,128)}, f32[32,128]{1,0:T(8,128)}, f32[1,64]{1,0:T(1,128)}, f32[64,64]{1,0:T(8,128)}) custom-call(f32[32,64]{1,0:T(8,128)S(1)} %get-tuple-element.15.refs_0_, f32[32,256]{1,0:T(8,128)S(1)} %get-tuple-element.16.refs_1_, f32[32,128]{1,0:T(8,128)S(1)} %get-tuple-element.17.refs_2_, ...), custom_call_target="tpu_custom_call" | custom-call | tf_op jit(solution)/shard_map/put/pallas_call | solution.py:468

commit v6 on v5

--- a/solution.py
+++ b/solution.py
@@ -58,6 +58,12 @@
 
     def arrived(ref, n, sem):
         pltpu.make_async_copy(ref.at[pl.ds(0, n)], ref.at[pl.ds(0, n)], sem).wait()
+
+    def hops(k, n):
+        return min(k, n - k)
+
+    far_sim = sorted(range(1, n_sim), key=lambda k: -hops(k // 4, 4) - hops(k % 4, 4))
+    far_sec = sorted(range(1, n_sec), key=lambda k: -hops(k, n_sec))
 
     small = [
         pltpu.make_async_copy(counts_hbm, counts, int_sem.at[0]),
@@ -107,7 +113,6 @@
         sel[:, 128 * r:128 * (r + 1)] = jnp.where(
             row128 == (col128 // width) * width + 4 * me + r, 1.0, 0.0
         ).astype(BF16)
-    gsend[...] = jnp.zeros((8 * n_sim, 128), F32)
 
     lane_c = iota((1, cells), 1)
     left64 = iota((width, 128), 1) < width
@@ -142,6 +147,52 @@
 
     staged = first_x.shape[1]
     qsum = jnp.zeros((width, 128), F32)
+    def both_sides(value):
+        turned = pltpu.roll(value, width, 1)
+        return jnp.where(left16, value, turned), jnp.where(left16, turned, value)
+
+    def about(m_even, m_odd, w_even, w_odd):
+        count = jnp.sum(w_even + w_odd, axis=0, keepdims=True)
+        mean = jnp.sum(w_even * m_even + w_odd * m_odd, axis=0, keepdims=True) / jnp.maximum(count, 1.0)
+        d_even, d_odd = m_even - mean, m_odd - mean
+        off = jnp.concatenate([d_even, d_odd], axis=0)
+        left = jnp.concatenate([w_even * d_even, w_odd * d_odd], axis=0)
+        return count, mean, outer_sum(left, off)[0:width, :]
+
+    def here(c, d):
+        return jnp.clip(c - d * cells, 0, cells).astype(F32)
+
+    lane32, sub32 = iota((width // 2, 128), 1), iota((width // 2, 128), 0)
+    left32 = lane32 < width
+    col32 = lane32 % width
+    inner32 = col32 < width // 2
+    above32 = col32 > sub32
+
+    def folded(m, mean, count):
+        top, bottom = m[0:width // 2, :], m[width // 2:width, :]
+        kept = jnp.where(inner32 & ~above32, pltpu.roll(bottom, width // 2, 1), top)
+        diagonal = jnp.sum(jnp.where(col32 == sub32, top, 0.0), axis=0, keepdims=True)
+        info = jnp.where(sub8 == 0, mean, jnp.where(sub8 == 1, count, jnp.where(sub8 == 2, diagonal, 0.0)))
+        quarter = width // 4
+        return jnp.concatenate(
+            [jnp.where(left16, kept[0:quarter, :], kept[quarter:2 * quarter, :]), info], axis=0
+        )
+
+    def unfolded(m):
+        swapped = pltpu.roll(m[0:pairs, :], width, 1)
+        kept = jnp.concatenate(
+            [jnp.where(left16, m[0:pairs, :], swapped), jnp.where(left16, swapped, m[0:pairs, :])], axis=0
+        )
+        turned = jnp.concatenate([kept, kept, kept, kept], axis=0).T[0:width, :]
+        first = jnp.where(above32, kept, jnp.where(col32 == sub32, m[pairs + 2:pairs + 3, :], turned[0:width // 2, :]))
+        top = jnp.where(inner32, first, kept)
+        last = pltpu.roll(jnp.where(above32, turned[0:width // 2, :], kept), width // 2, 1)
+        bottom = jnp.where(inner32, turned[width // 2:, :], last)
+        return jnp.concatenate([top, bottom], axis=0)
+
+    def third(i):
+        return pl.ds(pl.multiple_of(24 * i, 8), 24)
+
     for i in range(half + 1):
         if i == 0 or i % 2 == 1:
             for p in range(i, min(half, i + 1 + i % 2)):
@@ -149,12 +200,24 @@
                 loads[p + half].wait()
         if i < half:
             centre(i)
-        if i > 0:
+        if i > 0 and i != half - 1:
+            if i == half:
+                qsum = multiply(i - 2, qsum)
             qsum = multiply(i - 1, qsum)
-        if i == half - 1:
+        if i == half:
             mine = colsum[...].T[0:pairs, :]
             sums[me] = mine
-            for k in range(1, n_sim):
+            n_mine = here(n_int, me)
+            l_even, l_odd = both_sides(mine / jnp.maximum(n_mine, 1.0))
+            dev_count, dev_mean, dev_co = about(l_even, l_odd, here(c_even, me), here(c_odd, me))
+            q = qsum + pltpu.roll(qsum, width, 1) + dev_co
+            fold[...] = folded(q, dev_mean, dev_count)
+            for k in far_sec:
+                pltpu.make_async_remote_copy(
+                    fold, qrecv.at[third(sec), :], send_sem.at[2], q_sem,
+                    device_id=(sec_peer(k), me), device_id_type=MESH,
+                ).start()
+            for k in far_sim:
                 pltpu.make_async_remote_copy(
                     sums.at[me], sums.at[me], send_sem.at[0], sums_sem,
                     device_id=(sec, sim_peer(k)), device_id_type=MESH,
@@ -176,70 +239,13 @@
                         device_id=(sec, to * 4 + x), device_id_type=MESH,
                     ).start()
             else:
-                for k in range(1, n_sim):
+                for k in far_sim:
                     pltpu.make_async_remote_copy(
                         sendb.at[pl.ds(i - 2, 2), along_z(k // 4), block(along_x(k % 4)), :],
                         straight.at[k - 1, t - staged],
                         send_sem.at[5], straight_sem.at[t - staged],
                         device_id=(sec, sim_peer(k)), device_id_type=MESH,
                     ).start()
-    def both_sides(value):
-        turned = pltpu.roll(value, width, 1)
-        return jnp.where(left16, value, turned), jnp.where(left16, turned, value)
-
-    def about(m_even, m_odd, w_even, w_odd):
-        count = jnp.sum(w_even + w_odd, axis=0, keepdims=True)
-        mean = jnp.sum(w_even * m_even + w_odd * m_odd, axis=0, keepdims=True) / jnp.maximum(count, 1.0)
-        d_even, d_odd = m_even - mean, m_odd - mean
-        off = jnp.concatenate([d_even, d_odd], axis=0)
-        left = jnp.concatenate([w_even * d_even, w_odd * d_odd], axis=0)
-        return count, mean, outer_sum(left, off)[0:width, :]
-
-    def here(c, d):
-        return jnp.clip(c - d * cells, 0, cells).astype(F32)
-
-    n_mine = here(n_int, me)
-    l_even, l_odd = both_sides(mine / jnp.maximum(n_mine, 1.0))
-    dev_count, dev_mean, dev_co = about(l_even, l_odd, here(c_even, me), here(c_odd, me))
-    q = qsum + pltpu.roll(qsum, width, 1) + dev_co
-
-    lane32, sub32 = iota((width // 2, 128), 1), iota((width // 2, 128), 0)
-    left32 = lane32 < width
-    col32 = lane32 % width
-    inner32 = col32 < width // 2
-    above32 = col32 > sub32
-
-    def folded(m, mean, count):
-        top, bottom = m[0:width // 2, :], m[width // 2:width, :]
-        kept = jnp.where(inner32 & ~above32, pltpu.roll(bottom, width // 2, 1), top)
-        diagonal = jnp.sum(jnp.where(col32 == sub32, top, 0.0), axis=0, keepdims=True)
-        info = jnp.where(sub8 == 0, mean, jnp.where(sub8 == 1, count, jnp.where(sub8 == 2, diagonal, 0.0)))
-        quarter = width // 4
-        return jnp.concatenate(
-            [jnp.where(left16, kept[0:quarter, :], kept[quarter:2 * quarter, :]), info], axis=0
-        )
-
-    def unfolded(m):
-        swapped = pltpu.roll(m[0:pairs, :], width, 1)
-        kept = jnp.concatenate(
-            [jnp.where(left16, m[0:pairs, :], swapped), jnp.where(left16, swapped, m[0:pairs, :])], axis=0
-        )
-        turned = jnp.concatenate([kept, kept, kept, kept], axis=0).T[0:width, :]
-        first = jnp.where(above32, kept, jnp.where(col32 == sub32, m[pairs + 2:pairs + 3, :], turned[0:width // 2, :]))
-        top = jnp.where(inner32, first, kept)
-        last = pltpu.roll(jnp.where(above32, turned[0:width // 2, :], kept), width // 2, 1)
-        bottom = jnp.where(inner32, turned[width // 2:, :], last)
-        return jnp.concatenate([top, bottom], axis=0)
-
-    def third(i):
-        return pl.ds(pl.multiple_of(24 * i, 8), 24)
-
-    fold[...] = folded(q, dev_mean, dev_count)
-    for k in range(1, n_sec):
-        pltpu.make_async_remote_copy(
-            fold, qrecv.at[third(sec), :], send_sem.at[2], q_sem,
-            device_id=(sec_peer(k), me), device_id_type=MESH,
-        ).start()
     qrecv[third(sec), :] = fold[...]
 
     lane64, sub64 = iota((width, 128), 1), iota((width, 128), 0)
@@ -283,7 +289,7 @@
     extra = folded(part_co, part_mean, part_count)
     info = jnp.where(sub8 == 2, part[pairs:, :] + extra[pairs:, :], extra[pairs:, :])
     zrecv[third(me), :] = jnp.concatenate([part[0:pairs, :] + extra[0:pairs, :], info], axis=0)
-    for k in range(1, n_sim):
+    for k in far_sim:
         pltpu.make_async_remote_copy(
             zrecv.at[third(me), :], zrecv.at[third(me), :], send_sem.at[3], z_sem,
             device_id=(sec, sim_peer(k)), device_id_type=MESH,
@@ -315,14 +321,6 @@
         for pp in range(2):
             corrb[pl.ds(2 * r + pp, half, stride=8), :] = rows[half * pp:half * (pp + 1), :]
     co = corrb[...]
-    m_even, m_odd = both_sides(means)
-    grp_count, _, grp_co = about(
-        m_even, m_odd,
-        jnp.where(o_even == me, c_even, 0).astype(F32), jnp.where(o_odd == me, c_odd, 0).astype(F32),
-    )
-    corrb[...] = grp_co
-    between = jnp.where(left32, corrb[pl.ds(0, width // 2, stride=2), :], corrb[pl.ds(1, width // 2, stride=2), :])
-
     pltpu.make_async_copy(second_x, second_x, second_sem.at[0]).wait()
     pltpu.make_async_copy(second_z, second_z, second_sem.at[1]).wait()
     tiles = []
@@ -343,15 +341,23 @@
     named = jnp.dot(names, jnp.concatenate([top, low], axis=0), preferred_element_type=F32)
     g = jnp.where(left64, named[0:width, :], named[width:, :])
     g = g + pltpu.roll(g, width, 1)
-    gsend[pl.ds(0, n_sim, stride=8), :] = jnp.where(left16, g[0:16, :], g[16:32, :])
-    gsend[pl.ds(1, n_sim, stride=8), :] = jnp.where(left16, g[32:48, :], g[48:64, :])
-    for k in range(1, n_sim):
+    gsend[:, 0, :] = jnp.where(left16, g[0:16, :], g[16:32, :])
+    gsend[:, 1, :] = jnp.where(left16, g[32:48, :], g[48:64, :])
+    for k in far_sim:
         to = sim_peer(k)
         pltpu.make_async_remote_copy(
-            gsend.at[block(to), :], grecv.at[block(me), :], send_sem.at[4], g_sem,
+            gsend.at[to], grecv.at[me], send_sem.at[4], g_sem,
             device_id=(sec, to), device_id_type=MESH,
         ).start()
-    grecv[block(me), :] = gsend[block(me), :]
+    grecv[me] = gsend[me]
+
+    m_even, m_odd = both_sides(means)
+    grp_count, _, grp_co = about(
+        m_even, m_odd,
+        jnp.where(o_even == me, c_even, 0).astype(F32), jnp.where(o_odd == me, c_odd, 0).astype(F32),
+    )
+    corrb[...] = grp_co
+    between = jnp.where(left32, corrb[pl.ds(0, width // 2, stride=2), :], corrb[pl.ds(1, width // 2, stride=2), :])
 
     arrived(zrecv, 24 * (n_sim - 1), z_sem)
     part, all_mean, all_count, all_co = merged(zrecv, n_sim)
@@ -369,9 +375,9 @@
     cov_out[:, 0:128] = turn[...]
     cov_out[:, 128:256] = turn2[...]
 
-    arrived(grecv, 8 * (n_sim - 1), g_sem)
-    grp[pl.ds(0, n_sim, stride=2), :] = grecv[pl.ds(0, n_sim, stride=8), :]
-    grp[pl.ds(1, n_sim, stride=2), :] = grecv[pl.ds(1, n_sim, stride=8), :]
+    arrived(grecv, n_sim - 1, g_sem)
+    grp[pl.ds(0, n_sim, stride=2), :] = grecv[:, 0, :]
+    grp[pl.ds(1, n_sim, stride=2), :] = grecv[:, 1, :]
     grp_out[...] = (grp[...] + between) / jnp.maximum(grp_count - 1.0, 1.0)
 
     arrived(sums, n_sim - 1, send_sem.at[0])
@@ -379,7 +385,7 @@
     arrived(first_z, 3, send_sem.at[7])
     arrived(qrecv, 24 * (n_sec - 1), send_sem.at[2])
     arrived(zrecv, 24 * (n_sim - 1), send_sem.at[3])
-    arrived(grecv, 8 * (n_sim - 1), send_sem.at[4])
+    arrived(grecv, n_sim - 1, send_sem.at[4])
     arrived(straight, n_sim - 1, send_sem.at[5])
     arrived(second_x, 3, send_sem.at[6])
     arrived(second_z, 3, send_sem.at[8])
@@ -436,8 +442,8 @@
                 pltpu.VMEM((24, 128), F32),
                 pltpu.VMEM((24 * n_sec, 128), F32),
                 pltpu.VMEM((24 * n_sim, 128), F32),
-                pltpu.VMEM((8 * n_sim, 128), F32),
-                pltpu.VMEM((8 * n_sim, 128), F32),
+                pltpu.VMEM((n_sim, 2, 128), F32),
+                pltpu.VMEM((n_sim, 2, 128), F32),
                 pltpu.VMEM((width // 2, 128), F32),
                 pltpu.VMEM((width, 128), F32),
                 pltpu.VMEM((width, 128), F32),

time: 23.5 us -> 22.9 us (0.974)
  Pallas kernels: 22.7 us -> 22.2 us
    pallas_call x1, Pallas kernels: 22 us -> 21.5 us  [local(): pl.pallas_call(functools.partial(kernel, n_sec, n_sim, width), out_shape=...]
where the time goes in v6:
time: 22.9 us; the launch traced here: 22.8 us
  Pallas kernels  22.2 us (97%)
  between operations  0.64 us (3%)
    pallas_call x1, Pallas kernels, local(): pl.pallas_call(functools.partial(kernel, n_sec, n_sim, width), out_shape=...  21.5 us
    pallas_call x1, Pallas kernels, local(): pl.pallas_call(functools.partial(put, 5), out_shape=shapes, in_specs=[vme...  0.69 us

profile of v6, /device:TPU:1, one launch (start us, length us, event | category | flops | bytes accessed | tf_op | source)
XLA Modules:
  0.0 22.8 jit_solution(3200677583189651186)
XLA Ops:
  0.6 21.5 %moments.1 = (f32[32,64]{1,0:T(8,128)S(1)}, f32[32,256]{1,0:T(8,128)S(1)}, f32[32,128]{1,0:T(8,128)S(1)}, f32[1,64]{1,0:T(1,128)S(1)}, f32[64,64]{1,0:T(8,128)S(1)}) custom-call(f32[16,128,1024]{2,1,0:T(8,128)} %bitcast.4, s32[32]{0:T(128)} %counts_hbm.1, s32[32]{0:T(128)} %bitcast.5), custom_call_target="tpu_custom_call" | custom-call | tf_op jit(solution)/shard_map/moments/pallas_call | solution.py:422
  22.1 0.7 %put.1 = (f32[32,64]{1,0:T(8,128)}, f32[32,256]{1,0:T(8,128)}, f32[32,128]{1,0:T(8,128)}, f32[1,64]{1,0:T(1,128)}, f32[64,64]{1,0:T(8,128)}) custom-call(f32[32,64]{1,0:T(8,128)S(1)} %get-tuple-element.15.refs_0_, f32[32,256]{1,0:T(8,128)S(1)} %get-tuple-element.16.refs_1_, f32[32,128]{1,0:T(8,128)S(1)} %get-tuple-element.17.refs_2_, ...), custom_call_target="tpu_custom_call" | custom-call | tf_op jit(solution)/shard_map/put/pallas_call | solution.py:474

commit v7 on v6

--- a/solution.py
+++ b/solution.py
@@ -123,9 +123,10 @@
             for h in range(2):
                 n = jnp.clip(counts[2 * p + h] - base, 0, cells)
                 live = lane_c < n
+                weight = jnp.where(live, 1.0, 0.0)
                 for r in range(h * width, (h + 1) * width, 16):
                     cell = xv[p, r:r + 16, :]
-                    s = jnp.sum(jnp.where(live, cell, 0.0), axis=1, keepdims=True)
+                    s = jnp.sum(cell * weight, axis=1, keepdims=True)
                     colsum[r:r + 16, p:p + 1] = s
                     m = s / jnp.maximum(n, 1).astype(F32)
                     c = jnp.where(live, cell - m, 0.0)
@@ -210,6 +211,11 @@
             n_mine = here(n_int, me)
             l_even, l_odd = both_sides(mine / jnp.maximum(n_mine, 1.0))
             dev_count, dev_mean, dev_co = about(l_even, l_odd, here(c_even, me), here(c_odd, me))
+            for k in far_sim:
+                pltpu.make_async_remote_copy(
+                    sums.at[me], sums.at[me], send_sem.at[0], sums_sem,
+                    device_id=(sec, sim_peer(k)), device_id_type=MESH,
+                ).start()
             q = qsum + pltpu.roll(qsum, width, 1) + dev_co
             fold[...] = folded(q, dev_mean, dev_count)
             for k in far_sec:
@@ -217,17 +223,12 @@
                     fold, qrecv.at[third(sec), :], send_sem.at[2], q_sem,
                     device_id=(sec_peer(k), me), device_id_type=MESH,
                 ).start()
-            for k in far_sim:
-                pltpu.make_async_remote_copy(
-                    sums.at[me], sums.at[me], send_sem.at[0], sums_sem,
-                    device_id=(sec, sim_peer(k)), device_id_type=MESH,
-                ).start()
         if i > 0 and i % 2 == 0:
             t = i // 2 - 1
             if t == 0:
                 pl.semaphore_wait(barrier, n_sim - 1 + n_sec - 1)
             if t < staged:
-                for k in range(1, 4):
+                for k in (2, 1, 3):
                     to = along_x(k)
                     pltpu.make_async_remote_copy(
                         sendb.at[i - 2, :, block(to), :], first_x.at[k - 1, t], send_sem.at[1], first_sem.at[t, 0],
@@ -272,7 +273,7 @@
         pltpu.make_async_copy(few, few, first_sem.at[t, 1]).wait()
         part_x[t] = sendb[2 * t, :, block(x), :] + first_x[0, t] + first_x[1, t] + first_x[2, t]
         part_z[t] = sendb[2 * t + 1, z] + first_z[0, t] + first_z[1, t] + first_z[2, t]
-    for k in range(1, 4):
+    for k in (2, 1, 3):
         to = along_z(k)
         pltpu.make_async_remote_copy(
             part_x.at[:, to], second_x.at[k - 1], send_sem.at[6], second_sem.at[0],

time: 22.9 us -> 22.9 us (level)
  no operation moved by 1% of the time
where the time goes in v7:
time: 22.9 us; the launch traced here: 22.8 us
  Pallas kernels  22.1 us (97%)
  between operations  0.64 us (3%)
    pallas_call x1, Pallas kernels, local(): pl.pallas_call(functools.partial(kernel, n_sec, n_sim, width), out_shape=...  21.4 us
    pallas_call x1, Pallas kernels, local(): pl.pallas_call(functools.partial(put, 5), out_shape=shapes, in_specs=[vme...  0.69 us

profile of v7, /device:TPU:1, one launch (start us, length us, event | category | flops | bytes accessed | tf_op | source)
XLA Modules:
  0.0 22.8 jit_solution(9216470139272321946)
XLA Ops:
  0.6 21.4 %moments.1 = (f32[32,64]{1,0:T(8,128)S(1)}, f32[32,256]{1,0:T(8,128)S(1)}, f32[32,128]{1,0:T(8,128)S(1)}, f32[1,64]{1,0:T(1,128)S(1)}, f32[64,64]{1,0:T(8,128)S(1)}) custom-call(f32[16,128,1024]{2,1,0:T(8,128)} %bitcast.4, s32[32]{0:T(128)} %counts_hbm.1, s32[32]{0:T(128)} %bitcast.5), custom_call_target="tpu_custom_call" | custom-call | tf_op jit(solution)/shard_map/moments/pallas_call | solution.py:423
  22.1 0.7 %put.1 = (f32[32,64]{1,0:T(8,128)}, f32[32,256]{1,0:T(8,128)}, f32[32,128]{1,0:T(8,128)}, f32[1,64]{1,0:T(1,128)}, f32[64,64]{1,0:T(8,128)}) custom-call(f32[32,64]{1,0:T(8,128)S(1)} %get-tuple-element.15.refs_0_, f32[32,256]{1,0:T(8,128)S(1)} %get-tuple-element.16.refs_1_, f32[32,128]{1,0:T(8,128)S(1)} %get-tuple-element.17.refs_2_, ...), custom_call_target="tpu_custom_call" | custom-call | tf_op jit(solution)/shard_map/put/pallas_call | solution.py:475
